TPU v7x, 32 devices: a 4x4x1 block of a 4x4x8 slice. The times are simulated.
32 devices in a mesh: dp: 1 (over z), seq: 32 (over y, x, core).
Axes of the slice: x: 4, y: 4, z: 1, core: 2. Of those that a mesh axis runs over, the one named last changes fastest.
The devices are a block of a 4x4x8 slice.
Arguments:
- enc_out: bfloat16 [32, 64, 1024], P('dp', 'seq')
- pred_out: bfloat16 [32, 64, 640], P('dp')
- w_enc: bfloat16 [1024, 640], replicated
- w_pred: bfloat16 [640, 640], replicated
- w_out: bfloat16 [640, 1024], replicated
- labels: int32 [32, 63], P('dp')
- frame_len: int32 [32], P('dp')
- label_len: int32 [32], P('dp')
Outputs:
- output 1: float32 [32], P('dp')
- output 2: bfloat16 [32, 64, 1024], P('dp', 'seq')
- output 3: float32 [1024, 640], P('dp')
- output 4: float32 [640, 640], P('dp')
- output 5: float32 [640, 1024], P('dp')
All inputs are finite; a program needn't handle non-finite values.
Results may differ from a plain program's by a relative error of at most 0.0138273.
Values are sent between devices in bfloat16 or wider.
A program may use at most 768 MiB of HBM per device.

v0:
```python
import jax
import jax.numpy as jnp
from jax import lax
from jax.sharding import PartitionSpec as P

NEG_FILL = -1.0e30


def label_prefix(lab_lp):
    zero_col = jnp.zeros_like(lab_lp[:, :1])
    return jnp.concatenate([zero_col, jnp.cumsum(lab_lp[:, :-1], axis=1)], axis=1)


def label_weights(labels, w_out):
    n_utt = labels.shape[0]
    lab_ids = jnp.concatenate([labels, jnp.full((n_utt, 1), -1, jnp.int32)], axis=1)
    onehot = (lab_ids[:, :, None] == lax.broadcasted_iota(jnp.int32, (1, 1, w_out.shape[1]), 2)).astype(jnp.bfloat16)
    lab_w = jnp.einsum('buv,jv->buj', onehot, w_out, preferred_element_type=jnp.float32).astype(jnp.bfloat16)
    return lab_ids, lab_w


def joint_lattice(enc_blk, act_g, lab_w, w_enc, w_out):
    act_f = jnp.einsum('bth,hj->btj', enc_blk, w_enc, preferred_element_type=jnp.float32).astype(jnp.bfloat16)
    hidden = jnp.tanh(act_f[:, :, None, :].astype(jnp.float32) + act_g[:, None, :, :].astype(jnp.float32)).astype(jnp.bfloat16)
    logits = jnp.einsum('btuj,jv->btuv', hidden, w_out, preferred_element_type=jnp.float32)
    log_norm = jax.nn.logsumexp(logits, axis=-1)
    soft_probs = jnp.exp(logits - log_norm[..., None])
    blank_lp = logits[..., 0] - log_norm
    lab_lp = jnp.einsum('btuj,buj->btu', hidden, lab_w, preferred_element_type=jnp.float32) - log_norm
    return hidden, soft_probs, blank_lp, lab_lp


def alpha_rows(x_in, blank_lp, lab_lp):
    def frame_step(x_prev, frame_in):
        frame_blank, frame_lab = frame_in
        lab_sum = label_prefix(frame_lab)
        alpha_t = lab_sum + lax.cumlogsumexp(x_prev - lab_sum, axis=1)
        return alpha_t + frame_blank, alpha_t
    x_out, alphas = lax.scan(frame_step, x_in, (jnp.swapaxes(blank_lp, 0, 1), jnp.swapaxes(lab_lp, 0, 1)))
    return x_out, jnp.swapaxes(alphas, 0, 1)


def beta_rows(next_in, blank_lp, lab_lp, frame_ids, frame_len, boundary):
    def frame_step(next_row, frame_in):
        frame_blank, frame_lab, frame_id = frame_in
        lab_sum = label_prefix(frame_lab)
        beta_row = lax.cumlogsumexp(next_row + frame_blank + lab_sum, axis=1, reverse=True) - lab_sum
        beta_row = jnp.where((frame_id >= frame_len)[:, None], boundary, beta_row)
        return beta_row, (beta_row, next_row)
    first_row, (betas, beta_next) = lax.scan(frame_step, next_in, (jnp.swapaxes(blank_lp, 0, 1), jnp.swapaxes(lab_lp, 0, 1), frame_ids), reverse=True)
    return first_row, jnp.swapaxes(betas, 0, 1), jnp.swapaxes(beta_next, 0, 1)


def occupancy(alphas, betas, beta_next, blank_lp, lab_lp, log_prob, frame_ok):
    beta_up = jnp.concatenate([betas[:, :, 1:], jnp.full_like(betas[:, :, :1], NEG_FILL)], axis=2)
    norm_shift = log_prob[:, None, None]
    occ_blank = jnp.where(frame_ok, jnp.exp(jnp.minimum(alphas + blank_lp + beta_next - norm_shift, 0.0)), 0.0)
    occ_lab = jnp.where(frame_ok, jnp.exp(jnp.minimum(alphas + lab_lp + beta_up - norm_shift, 0.0)), 0.0)
    return occ_blank, occ_lab


def joint_backward(enc_blk, hidden, soft_probs, occ_blank, occ_lab, lab_ids, w_enc, w_out):
    vocab_ids = lax.broadcasted_iota(jnp.int32, (1, 1, 1, soft_probs.shape[-1]), 3)
    d_logits = (soft_probs * (occ_blank + occ_lab)[..., None] - jnp.where(vocab_ids == 0, occ_blank[..., None], 0.0) - jnp.where(vocab_ids == lab_ids[:, None, :, None], occ_lab[..., None], 0.0)).astype(jnp.bfloat16)
    d_hidden = jnp.einsum('btuv,jv->btuj', d_logits, w_out, preferred_element_type=jnp.float32)
    d_pre = (d_hidden * (1.0 - jnp.square(hidden.astype(jnp.float32)))).astype(jnp.bfloat16)
    d_act_f = jnp.sum(d_pre, axis=2, dtype=jnp.float32).astype(jnp.bfloat16)
    d_act_g = jnp.sum(d_pre, axis=1, dtype=jnp.float32)
    grad_enc = jnp.einsum('btj,hj->bth', d_act_f, w_enc, preferred_element_type=jnp.float32).astype(jnp.bfloat16)
    gw_enc = jnp.einsum('bth,btj->hj', enc_blk, d_act_f, preferred_element_type=jnp.float32)
    gw_out = jnp.einsum('btuj,btuv->jv', hidden, d_logits, preferred_element_type=jnp.float32)
    return grad_enc, gw_enc, gw_out, d_act_g


def solution(mesh):
    seq_size = mesh.shape['seq']
    fwd_pairs = [(src, src + 1) for src in range(seq_size - 1)]
    bwd_pairs = [(src + 1, src) for src in range(seq_size - 1)]

    def local_fn(enc_out, pred_out, w_enc, w_pred, w_out, labels, frame_len, label_len):
        seq_idx = lax.axis_index('seq')
        n_utt, n_loc, _ = enc_out.shape
        lab_pos = pred_out.shape[1]
        lab_ids, lab_w = label_weights(labels, w_out)
        act_g = jnp.einsum('buh,hj->buj', pred_out, w_pred, preferred_element_type=jnp.float32).astype(jnp.bfloat16)
        hidden, soft_probs, blank_lp, lab_lp = joint_lattice(enc_out, act_g, lab_w, w_enc, w_out)
        pos_ids = lax.broadcasted_iota(jnp.int32, (n_utt, lab_pos), 1)
        neg_rows = jnp.full((n_utt, lab_pos), NEG_FILL, jnp.float32)
        init_x = jnp.where(pos_ids == 0, 0.0, neg_rows)
        boundary = jnp.where(pos_ids == label_len[:, None], 0.0, neg_rows)
        frame_ids = seq_idx * n_loc + jnp.arange(n_loc, dtype=jnp.int32)

        def alpha_hop(hop_idx, x_in):
            x_out, _ = alpha_rows(x_in, blank_lp, lab_lp)
            received = lax.ppermute(x_out, 'seq', fwd_pairs)
            return jnp.where(seq_idx == 0, init_x, received)

        x_in = lax.fori_loop(0, seq_size - 1, alpha_hop, init_x)
        _, alphas = alpha_rows(x_in, blank_lp, lab_lp)

        def beta_hop(hop_idx, next_in):
            first_row, _, _ = beta_rows(next_in, blank_lp, lab_lp, frame_ids, frame_len, boundary)
            received = lax.ppermute(first_row, 'seq', bwd_pairs)
            return jnp.where(seq_idx == seq_size - 1, boundary, received)

        next_in = lax.fori_loop(0, seq_size - 1, beta_hop, boundary)
        first_row, betas, beta_next = beta_rows(next_in, blank_lp, lab_lp, frame_ids, frame_len, boundary)
        log_prob = lax.psum(jnp.where(seq_idx == 0, first_row[:, 0], 0.0), 'seq')
        frame_ok = (frame_ids[None, :] < frame_len[:, None])[:, :, None]
        occ_blank, occ_lab = occupancy(alphas, betas, beta_next, blank_lp, lab_lp, log_prob, frame_ok)
        grad_enc, gw_enc, gw_out, d_act_g = joint_backward(enc_out, hidden, soft_probs, occ_blank, occ_lab, lab_ids, w_enc, w_out)
        gw_pred = jnp.einsum('buh,buj->hj', pred_out, d_act_g, preferred_element_type=jnp.float32)
        gw_enc, gw_pred, gw_out = lax.psum((gw_enc, gw_pred, gw_out), 'seq')
        return -log_prob, grad_enc, gw_enc, gw_pred, gw_out

    in_specs = (P('dp', 'seq', None), P('dp', None, None), P(None, None), P(None, None), P(None, None), P('dp', None), P('dp'), P('dp'))
    out_specs = (P('dp'), P('dp', 'seq', None), P('dp', None), P('dp', None), P('dp', None))
    return jax.shard_map(local_fn, mesh=mesh, in_specs=in_specs, out_specs=out_specs, check_vma=False)
```

profile of v0, /device:TPU:97, one launch (start us, length us, event | category | flops | bytes accessed | tf_op | source)
XLA Modules:
  0.0 1287.3 jit_solution(9256301540637250054)
XLA Ops:
  33.6 20.9 %fusion.12 = f32[32,64,1,2]{3,2,1,0:T(1,128)} fusion(bf16[32,2,64,640]{3,2,1,0:T(8,128)(2,1)S(1)} %tanh_convert_fusion, bf16[32,64,640,1]{2,1,0,3:T(8,128)(2,1)S(1)} %copy-done.9), kind=kOutput, calls=%fused_computation.35 | convolution fusion | flops 5242880 | bytes 7880704 | tf_op jit(solution)/shard_map/btuj,buj->btu/dot_general | solution.py:29
  70.1 309.0 %while.108 = (s32[]{:T(128)}, f32[32,64]{1,0:T(8,128)S(1)}, pred[]{:T(512)}, f32[32,2,64]{2,0,1:T(8,128)S(1)}, f32[32,2,64]{2,0,1:T(8,128)S(1)}, /*index=5*/f32[...) while((s32[]{:T(128)}, f32[32,64]{1,0:T(8,128)S(1)}, ...), condition=%wide.region_18.19_spmd.clone, body=%wide.region_13.18_spmd.clone.sunk | while | flops 1165380 | bytes 155707 | solution.py:98
  382.9 665.8 %while.105 = (s32[]{:T(128)}, f32[32,64]{1,0:T(8,128)S(1)}, pred[]{:T(512)}, f32[32,2,64]{2,0,1:T(8,128)S(1)}, f32[32,2,64]{2,0,1:T(8,128)S(1)}, /*index=5*/s32[...) while((s32[]{:T(128)}, f32[32,64]{1,0:T(8,128)S(1)}, ...), condition=%wide.region_7.8_spmd.clone, body=%wide.region_2.7_spmd.clone.sunk | while | flops 1175655 | bytes 172387 | solution.py:106
  405.2 14.1 %while.109 = (s32[]{:T(128)}, f32[32,64]{1,0:T(8,128)S(1)}, s32[2]{0:T(128)S(1)}, s32[32]{0:T(128)S(1)}, f32[2,32,64]{2,1,0:T(8,128)S(1)}, /*index=5*/f32[2,32,6...) while((s32[]{:T(128)}, f32[32,64]{1,0:T(8,128)S(1)}, s32[2]{0:T(128)S(1)}, ...), condition=%wide.region_6.6_spmd, body=%wide.region_3.5_spmd.sunk | while | flops 1165411 | bytes 114513 | solution.py:50
  426.4 14.1 %while.109 = (s32[]{:T(128)}, f32[32,64]{1,0:T(8,128)S(1)}, s32[2]{0:T(128)S(1)}, s32[32]{0:T(128)S(1)}, f32[2,32,64]{2,1,0:T(8,128)S(1)}, /*index=5*/f32[2,32,6...) while((s32[]{:T(128)}, f32[32,64]{1,0:T(8,128)S(1)}, s32[2]{0:T(128)S(1)}, ...), condition=%wide.region_6.6_spmd, body=%wide.region_3.5_spmd.sunk | while | flops 1165411 | bytes 114513 | solution.py:50
  448.4 14.1 %while.109 = (s32[]{:T(128)}, f32[32,64]{1,0:T(8,128)S(1)}, s32[2]{0:T(128)S(1)}, s32[32]{0:T(128)S(1)}, f32[2,32,64]{2,1,0:T(8,128)S(1)}, /*index=5*/f32[2,32,6...) while((s32[]{:T(128)}, f32[32,64]{1,0:T(8,128)S(1)}, s32[2]{0:T(128)S(1)}, ...), condition=%wide.region_6.6_spmd, body=%wide.region_3.5_spmd.sunk | while | flops 1165411 | bytes 114513 | solution.py:50
  469.6 14.1 %while.109 = (s32[]{:T(128)}, f32[32,64]{1,0:T(8,128)S(1)}, s32[2]{0:T(128)S(1)}, s32[32]{0:T(128)S(1)}, f32[2,32,64]{2,1,0:T(8,128)S(1)}, /*index=5*/f32[2,32,6...) while((s32[]{:T(128)}, f32[32,64]{1,0:T(8,128)S(1)}, s32[2]{0:T(128)S(1)}, ...), condition=%wide.region_6.6_spmd, body=%wide.region_3.5_spmd.sunk | while | flops 1165411 | bytes 114513 | solution.py:50
  491.6 14.1 %while.109 = (s32[]{:T(128)}, f32[32,64]{1,0:T(8,128)S(1)}, s32[2]{0:T(128)S(1)}, s32[32]{0:T(128)S(1)}, f32[2,32,64]{2,1,0:T(8,128)S(1)}, /*index=5*/f32[2,32,6...) while((s32[]{:T(128)}, f32[32,64]{1,0:T(8,128)S(1)}, s32[2]{0:T(128)S(1)}, ...), condition=%wide.region_6.6_spmd, body=%wide.region_3.5_spmd.sunk | while | flops 1165411 | bytes 114513 | solution.py:50
  512.9 14.1 %while.109 = (s32[]{:T(128)}, f32[32,64]{1,0:T(8,128)S(1)}, s32[2]{0:T(128)S(1)}, s32[32]{0:T(128)S(1)}, f32[2,32,64]{2,1,0:T(8,128)S(1)}, /*index=5*/f32[2,32,6...) while((s32[]{:T(128)}, f32[32,64]{1,0:T(8,128)S(1)}, s32[2]{0:T(128)S(1)}, ...), condition=%wide.region_6.6_spmd, body=%wide.region_3.5_spmd.sunk | while | flops 1165411 | bytes 114513 | solution.py:50
  534.9 14.1 %while.109 = (s32[]{:T(128)}, f32[32,64]{1,0:T(8,128)S(1)}, s32[2]{0:T(128)S(1)}, s32[32]{0:T(128)S(1)}, f32[2,32,64]{2,1,0:T(8,128)S(1)}, /*index=5*/f32[2,32,6...) while((s32[]{:T(128)}, f32[32,64]{1,0:T(8,128)S(1)}, s32[2]{0:T(128)S(1)}, ...), condition=%wide.region_6.6_spmd, body=%wide.region_3.5_spmd.sunk | while | flops 1165411 | bytes 114513 | solution.py:50
  556.3 14.1 %while.109 = (s32[]{:T(128)}, f32[32,64]{1,0:T(8,128)S(1)}, s32[2]{0:T(128)S(1)}, s32[32]{0:T(128)S(1)}, f32[2,32,64]{2,1,0:T(8,128)S(1)}, /*index=5*/f32[2,32,6...) while((s32[]{:T(128)}, f32[32,64]{1,0:T(8,128)S(1)}, s32[2]{0:T(128)S(1)}, ...), condition=%wide.region_6.6_spmd, body=%wide.region_3.5_spmd.sunk | while | flops 1165411 | bytes 114513 | solution.py:50
  577.7 14.1 %while.109 = (s32[]{:T(128)}, f32[32,64]{1,0:T(8,128)S(1)}, s32[2]{0:T(128)S(1)}, s32[32]{0:T(128)S(1)}, f32[2,32,64]{2,1,0:T(8,128)S(1)}, /*index=5*/f32[2,32,6...) while((s32[]{:T(128)}, f32[32,64]{1,0:T(8,128)S(1)}, s32[2]{0:T(128)S(1)}, ...), condition=%wide.region_6.6_spmd, body=%wide.region_3.5_spmd.sunk | while | flops 1165411 | bytes 114513 | solution.py:50
  599.1 14.1 %while.109 = (s32[]{:T(128)}, f32[32,64]{1,0:T(8,128)S(1)}, s32[2]{0:T(128)S(1)}, s32[32]{0:T(128)S(1)}, f32[2,32,64]{2,1,0:T(8,128)S(1)}, /*index=5*/f32[2,32,6...) while((s32[]{:T(128)}, f32[32,64]{1,0:T(8,128)S(1)}, s32[2]{0:T(128)S(1)}, ...), condition=%wide.region_6.6_spmd, body=%wide.region_3.5_spmd.sunk | while | flops 1165411 | bytes 114513 | solution.py:50
  620.5 14.1 %while.109 = (s32[]{:T(128)}, f32[32,64]{1,0:T(8,128)S(1)}, s32[2]{0:T(128)S(1)}, s32[32]{0:T(128)S(1)}, f32[2,32,64]{2,1,0:T(8,128)S(1)}, /*index=5*/f32[2,32,6...) while((s32[]{:T(128)}, f32[32,64]{1,0:T(8,128)S(1)}, s32[2]{0:T(128)S(1)}, ...), condition=%wide.region_6.6_spmd, body=%wide.region_3.5_spmd.sunk | while | flops 1165411 | bytes 114513 | solution.py:50
  641.9 14.1 %while.109 = (s32[]{:T(128)}, f32[32,64]{1,0:T(8,128)S(1)}, s32[2]{0:T(128)S(1)}, s32[32]{0:T(128)S(1)}, f32[2,32,64]{2,1,0:T(8,128)S(1)}, /*index=5*/f32[2,32,6...) while((s32[]{:T(128)}, f32[32,64]{1,0:T(8,128)S(1)}, s32[2]{0:T(128)S(1)}, ...), condition=%wide.region_6.6_spmd, body=%wide.region_3.5_spmd.sunk | while | flops 1165411 | bytes 114513 | solution.py:50
  663.3 14.1 %while.109 = (s32[]{:T(128)}, f32[32,64]{1,0:T(8,128)S(1)}, s32[2]{0:T(128)S(1)}, s32[32]{0:T(128)S(1)}, f32[2,32,64]{2,1,0:T(8,128)S(1)}, /*index=5*/f32[2,32,6...) while((s32[]{:T(128)}, f32[32,64]{1,0:T(8,128)S(1)}, s32[2]{0:T(128)S(1)}, ...), condition=%wide.region_6.6_spmd, body=%wide.region_3.5_spmd.sunk | while | flops 1165411 | bytes 114513 | solution.py:50
  684.7 14.1 %while.109 = (s32[]{:T(128)}, f32[32,64]{1,0:T(8,128)S(1)}, s32[2]{0:T(128)S(1)}, s32[32]{0:T(128)S(1)}, f32[2,32,64]{2,1,0:T(8,128)S(1)}, /*index=5*/f32[2,32,6...) while((s32[]{:T(128)}, f32[32,64]{1,0:T(8,128)S(1)}, s32[2]{0:T(128)S(1)}, ...), condition=%wide.region_6.6_spmd, body=%wide.region_3.5_spmd.sunk | while | flops 1165411 | bytes 114513 | solution.py:50
  706.1 14.1 %while.109 = (s32[]{:T(128)}, f32[32,64]{1,0:T(8,128)S(1)}, s32[2]{0:T(128)S(1)}, s32[32]{0:T(128)S(1)}, f32[2,32,64]{2,1,0:T(8,128)S(1)}, /*index=5*/f32[2,32,6...) while((s32[]{:T(128)}, f32[32,64]{1,0:T(8,128)S(1)}, s32[2]{0:T(128)S(1)}, ...), condition=%wide.region_6.6_spmd, body=%wide.region_3.5_spmd.sunk | while | flops 1165411 | bytes 114513 | solution.py:50
  727.6 14.1 %while.109 = (s32[]{:T(128)}, f32[32,64]{1,0:T(8,128)S(1)}, s32[2]{0:T(128)S(1)}, s32[32]{0:T(128)S(1)}, f32[2,32,64]{2,1,0:T(8,128)S(1)}, /*index=5*/f32[2,32,6...) while((s32[]{:T(128)}, f32[32,64]{1,0:T(8,128)S(1)}, s32[2]{0:T(128)S(1)}, ...), condition=%wide.region_6.6_spmd, body=%wide.region_3.5_spmd.sunk | while | flops 1165411 | bytes 114513 | solution.py:50
  749.0 14.1 %while.109 = (s32[]{:T(128)}, f32[32,64]{1,0:T(8,128)S(1)}, s32[2]{0:T(128)S(1)}, s32[32]{0:T(128)S(1)}, f32[2,32,64]{2,1,0:T(8,128)S(1)}, /*index=5*/f32[2,32,6...) while((s32[]{:T(128)}, f32[32,64]{1,0:T(8,128)S(1)}, s32[2]{0:T(128)S(1)}, ...), condition=%wide.region_6.6_spmd, body=%wide.region_3.5_spmd.sunk | while | flops 1165411 | bytes 114513 | solution.py:50
  770.4 14.1 %while.109 = (s32[]{:T(128)}, f32[32,64]{1,0:T(8,128)S(1)}, s32[2]{0:T(128)S(1)}, s32[32]{0:T(128)S(1)}, f32[2,32,64]{2,1,0:T(8,128)S(1)}, /*index=5*/f32[2,32,6...) while((s32[]{:T(128)}, f32[32,64]{1,0:T(8,128)S(1)}, s32[2]{0:T(128)S(1)}, ...), condition=%wide.region_6.6_spmd, body=%wide.region_3.5_spmd.sunk | while | flops 1165411 | bytes 114513 | solution.py:50
  791.8 14.1 %while.109 = (s32[]{:T(128)}, f32[32,64]{1,0:T(8,128)S(1)}, s32[2]{0:T(128)S(1)}, s32[32]{0:T(128)S(1)}, f32[2,32,64]{2,1,0:T(8,128)S(1)}, /*index=5*/f32[2,32,6...) while((s32[]{:T(128)}, f32[32,64]{1,0:T(8,128)S(1)}, s32[2]{0:T(128)S(1)}, ...), condition=%wide.region_6.6_spmd, body=%wide.region_3.5_spmd.sunk | while | flops 1165411 | bytes 114513 | solution.py:50
  813.2 14.1 %while.109 = (s32[]{:T(128)}, f32[32,64]{1,0:T(8,128)S(1)}, s32[2]{0:T(128)S(1)}, s32[32]{0:T(128)S(1)}, f32[2,32,64]{2,1,0:T(8,128)S(1)}, /*index=5*/f32[2,32,6...) while((s32[]{:T(128)}, f32[32,64]{1,0:T(8,128)S(1)}, s32[2]{0:T(128)S(1)}, ...), condition=%wide.region_6.6_spmd, body=%wide.region_3.5_spmd.sunk | while | flops 1165411 | bytes 114513 | solution.py:50
  834.6 14.1 %while.109 = (s32[]{:T(128)}, f32[32,64]{1,0:T(8,128)S(1)}, s32[2]{0:T(128)S(1)}, s32[32]{0:T(128)S(1)}, f32[2,32,64]{2,1,0:T(8,128)S(1)}, /*index=5*/f32[2,32,6...) while((s32[]{:T(128)}, f32[32,64]{1,0:T(8,128)S(1)}, s32[2]{0:T(128)S(1)}, ...), condition=%wide.region_6.6_spmd, body=%wide.region_3.5_spmd.sunk | while | flops 1165411 | bytes 114513 | solution.py:50
  877.4 14.1 %while.109 = (s32[]{:T(128)}, f32[32,64]{1,0:T(8,128)S(1)}, s32[2]{0:T(128)S(1)}, s32[32]{0:T(128)S(1)}, f32[2,32,64]{2,1,0:T(8,128)S(1)}, /*index=5*/f32[2,32,6...) while((s32[]{:T(128)}, f32[32,64]{1,0:T(8,128)S(1)}, s32[2]{0:T(128)S(1)}, ...), condition=%wide.region_6.6_spmd, body=%wide.region_3.5_spmd.sunk | while | flops 1165411 | bytes 114513 | solution.py:50
  941.7 14.1 %while.109 = (s32[]{:T(128)}, f32[32,64]{1,0:T(8,128)S(1)}, s32[2]{0:T(128)S(1)}, s32[32]{0:T(128)S(1)}, f32[2,32,64]{2,1,0:T(8,128)S(1)}, /*index=5*/f32[2,32,6...) while((s32[]{:T(128)}, f32[32,64]{1,0:T(8,128)S(1)}, s32[2]{0:T(128)S(1)}, ...), condition=%wide.region_6.6_spmd, body=%wide.region_3.5_spmd.sunk | while | flops 1165411 | bytes 114513 | solution.py:50
  963.1 14.1 %while.109 = (s32[]{:T(128)}, f32[32,64]{1,0:T(8,128)S(1)}, s32[2]{0:T(128)S(1)}, s32[32]{0:T(128)S(1)}, f32[2,32,64]{2,1,0:T(8,128)S(1)}, /*index=5*/f32[2,32,6...) while((s32[]{:T(128)}, f32[32,64]{1,0:T(8,128)S(1)}, s32[2]{0:T(128)S(1)}, ...), condition=%wide.region_6.6_spmd, body=%wide.region_3.5_spmd.sunk | while | flops 1165411 | bytes 114513 | solution.py:50
  1027.3 14.1 %while.109 = (s32[]{:T(128)}, f32[32,64]{1,0:T(8,128)S(1)}, s32[2]{0:T(128)S(1)}, s32[32]{0:T(128)S(1)}, f32[2,32,64]{2,1,0:T(8,128)S(1)}, /*index=5*/f32[2,32,6...) while((s32[]{:T(128)}, f32[32,64]{1,0:T(8,128)S(1)}, s32[2]{0:T(128)S(1)}, ...), condition=%wide.region_6.6_spmd, body=%wide.region_3.5_spmd.sunk | while | flops 1165411 | bytes 114513 | solution.py:50
  1048.7 14.5 %while.106 = (s32[]{:T(128)}, f32[32,64]{1,0:T(8,128)S(1)}, f32[2,32,64]{2,0,1:T(2,128)S(1)}, f32[2,32,64]{2,0,1:T(2,128)S(1)}, s32[2]{0:T(128)S(1)}, /*index=5*...) while((s32[]{:T(128)}, f32[32,64]{1,0:T(8,128)S(1)}, ...), condition=%wide.region_11.12_spmd.clone, body=%wide.region_8.11_spmd.clone.sunk | while | flops 1169507 | bytes 139249 | solution.py:50
  1063.3 67.1 %psum.28 = f32[32]{0:T(128)S(1)} all-reduce(f32[32]{0:T(128)S(1)} %select_reduce_fusion), channel_id=1, replica_groups=mesh['dp'=1,'seq'=32] {'seq'}, use_global_device_ids=true, to_apply=%region_12.13 | all-reduce | flops 32 | bytes 256 | tf_op jit(solution)/shard_map/psum | solution.py:108
  1144.1 14.5 %fusion.56 = (bf16[32,2,640]{2,1,0:T(2,128)(2,1)S(1)}, bf16[32,2,64,640]{3,2,1,0:T(8,128)(2,1)S(1)}) fusion(bf16[32,2,64,640]{3,2,1,0:T(8,128)(2,1)} %copy-done.1, bf16[640,1024]{1,0:T(8,128)(2,1)S(1)} %copy-done.7, f32[32,2,64,1024]{3,2,1,0:T(8,128)} %get-tuple-element.855, f32[32,2,64]{2,1,0:T(2,128)S(1)} %get-tuple-element.851, ...), kind=kOutput, calls=%fused_computation.89 | convolution fusion | flops 5413756928 | bytes 30819328 | tf_op jit(solution)/shard_map/btuv,jv->btuj/dot_general | solution.py:65
  1168.3 102.2 %all-reduce.9.cloned.1.call-done = (f32[1024,640]{0,1:T(8,128)}, f32[640,640]{0,1:T(8,128)}, f32[640,1024]{1,0:T(8,128)}) async-done(((f32[1024,640]{0,1:T(8,128)}, f32[640,640]{0,1:T(8,128)}, f32[640,1024]{1,0:T(8,128)}), (f32[1024,640]{0,1:T(8,128)}, f32[640,640]{0,1:T(8,128)}, f32[640,1024]{1,0:T(8,128)})) %all-reduce.9.cloned.1.call-update) | async-done | bytes 6881296 | tf_op jit(solution)/shard_map/psum | solution.py:113
  (1124 shorter events, 1262.7 us)
Async XLA Ops:
  7.2 1263.3 %all-reduce.9.cloned.1.call-start = ((), (), s32[]{:S(2)}) async-start(), calls=%async_computation | async-start | bytes 13762560 | tf_op jit(solution)/shard_map/psum | solution.py:113
  178.9 7.2 collective-permute-start
  189.6 7.2 collective-permute-start
  200.4 7.2 collective-permute-start
  211.1 7.2 collective-permute-start
  221.8 7.2 collective-permute-start
  232.5 7.2 collective-permute-start
  243.2 7.2 collective-permute-start
  253.9 7.2 collective-permute-start
  264.7 7.2 collective-permute-start
  275.4 7.2 collective-permute-start
  286.1 7.2 collective-permute-start
  296.8 7.2 collective-permute-start
  307.5 7.2 collective-permute-start
  318.3 7.2 collective-permute-start
  329.0 7.2 collective-permute-start
  339.7 7.2 collective-permute-start
  350.4 7.2 collective-permute-start
  361.1 7.2 collective-permute-start
  371.8 7.2 collective-permute-start
  397.3 7.8 collective-permute-start.1
  440.5 7.8 collective-permute-start.1
  483.7 7.8 collective-permute-start.1
  526.9 7.8 collective-permute-start.1
  548.9 7.2 collective-permute-start.1
  570.3 7.2 collective-permute-start.1
  591.7 7.2 collective-permute-start.1
  613.2 7.2 collective-permute-start.1
  677.4 7.2 collective-permute-start.1
  763.0 7.2 collective-permute-start.1
  912.9 7.2 collective-permute-start.1
  998.6 7.2 collective-permute-start.1
  (41 other events, 593.7 us)
Sparse Core Ops, SparseCore 0:
  1165.3 105.1 all-reduce.8
where the time goes:
time: 1300 us; the launch traced here: 1290 us
  other arithmetic  541 us (42%)
  waiting for transfers between devices  293 us (23%)
  starting transfers between devices  234 us (18%)
  matrix products  77.4 us (6%)
  blocking collectives  67.1 us (5%)
  local copies, waits for them, and re-layouts  58.1 us (4%)
  between operations  14.8 us (1%)
    another operation x64, other arithmetic, frame_step(): lax.cumlogsumexp(next_row + frame_blank + lab_sum, axis=1, reverse=True)  345 us
    ppermute x31, starting transfers between devices, alpha_hop(): received = lax.ppermute(x_out, 'seq', fwd_pairs)  173 us
    ppermute x31, waiting for transfers between devices, beta_hop(): received = lax.ppermute(first_row, 'seq', bwd_pairs)  164 us
    psum x1, waiting for transfers between devices, local_fn(): gw_enc, gw_pred, gw_out = lax.psum((gw_enc, gw_pred, gw_out), 'seq')  102 us
    another operation x64, other arithmetic, frame_step(): alpha_t = lab_sum + lax.cumlogsumexp(x_prev - lab_sum, axis=1)  87.1 us
    psum x1, blocking collectives, local_fn(): log_prob = lax.psum(jnp.where(seq_idx == 0, first_row[:, 0], 0.0), 'seq')  67.1 us
    ppermute x31, starting transfers between devices, beta_hop(): received = lax.ppermute(first_row, 'seq', bwd_pairs)  60.4 us
    ge x64, other arithmetic, frame_step(): beta_row = jnp.where((frame_id >= frame_len)[:, None], boundary, beta_row)  41.5 us
  transfers between devices with their start and end apart: 63, of which 63 were waited for; matrix products, arithmetic and copies ran while one was open for 0% of the time, Pallas kernels for 0%

commit v1 on v0

v1 whole, which is shorter than its diff:
```python
import functools

import jax
import jax.numpy as jnp
from jax import lax
from jax.experimental import pallas as pl
from jax.experimental.pallas import tpu as pltpu
from jax.sharding import PartitionSpec as P

NEG = -1.0e30
SIDE = 4
LANES = 128
BLK_T = 8
F32 = jnp.float32
BF16 = jnp.bfloat16


def dot(a, b, ca, cb):
    return lax.dot_general(a, b, (((ca,), (cb,)), ((), ())), preferred_element_type=F32)


def lse2(x, y):
    m = jnp.maximum(x, y)
    return m + jnp.log(1.0 + jnp.exp(-jnp.abs(x - y)))


def pieces_rows(rows, cols, parts):
    tiles = rows * cols // (8 * LANES)
    return -(-tiles // parts) * 8


class Comm:
    def __init__(self, send_sem, recv_sem):
        self.send_sem, self.recv_sem, self.used, self.sent = send_sem, recv_sem, 0, []

    def send(self, src, dst, dev):
        k = self.used
        self.used += 1
        cp = pltpu.make_async_remote_copy(src_ref=src, dst_ref=dst, send_sem=self.send_sem.at[k], recv_sem=self.recv_sem.at[k],
                                          device_id={'seq': dev}, device_id_type=pl.DeviceIdType.MESH)
        cp.start()
        self.sent.append(cp)
        return cp

    def drain(self):
        for cp in self.sent:
            cp.wait_send()
        self.sent = []


class Ring:
    def __init__(self, pos, dev_of):
        self.me, self.r, self.l, self.o = pos, (pos + 1) % SIDE, (pos + 3) % SIDE, (pos + 2) % SIDE
        self.right, self.left = dev_of(self.r), dev_of(self.l)


def rs_start(comm, ring, view, buf):
    return (comm.send(view(ring.o, 0), buf[0], ring.right), comm.send(view(ring.o, 1), buf[2], ring.left),
            comm.send(view(ring.r, 1), buf[1], ring.right), comm.send(view(ring.l, 0), buf[3], ring.left))


def rs_mid(comm, ring, view, buf, st):
    st[0].wait_recv()
    v = view(ring.r, 0)
    v[...] += buf[0][...]
    a = comm.send(v, buf[4], ring.right)
    st[1].wait_recv()
    v = view(ring.l, 1)
    v[...] += buf[2][...]
    b = comm.send(v, buf[5], ring.left)
    return st + (a, b)


def rs_end(ring, view, buf, st, out):
    for k in (2, 3, 4, 5):
        st[k].wait_recv()
    out(0, view(ring.me, 0)[...] + buf[4][...] + buf[3][...])
    out(1, view(ring.me, 1)[...] + buf[5][...] + buf[1][...])


def ag_start(comm, ring, whole):
    v = whole(ring.me)
    return (comm.send(v, v, ring.right), comm.send(v, v, ring.left))


def ag_mid(comm, ring, half, st):
    st[0].wait_recv()
    v = half(ring.l, 0)
    a = comm.send(v, v, ring.right)
    st[1].wait_recv()
    v = half(ring.r, 1)
    b = comm.send(v, v, ring.left)
    return (a, b)


def ag_end(st):
    st[0].wait_recv()
    st[1].wait_recv()


class AllReduce:
    def __init__(self, comm, pos, part, full, r0, r1, r2):
        self.comm, (self.core, x, y, dev) = comm, pos
        self.part, self.full, self.r0, self.r1, self.r2 = part, full, r0, r1, r2
        rx = Ring(x, lambda i: dev(i, y, self.core))
        ry = Ring(y, lambda i: dev(x, i, self.core))
        self.rings = ((rx, ry), (ry, rx))
        self.sibling = dev(x, y, 1 - self.core)
        n = part.shape[4]
        h = n // 16 * 8
        self.cut = ((0, h), (h, n - h))

    def v1(self, ref, k):
        return lambda a, half: ref.at[self.core, k, a, pl.ds(2 * half, 2)]

    def v2(self, ref, k):
        return lambda b, half: ref.at[self.core, k, self.rings[k][0].me, b, pl.ds(*self.cut[half])]

    def b1(self, k):
        return [self.r1.at[k, s] for s in range(6)]

    def b2(self, k):
        return [self.r2.at[k, s, pl.ds(*self.cut[h])] for s, h in enumerate((0, 1, 1, 0, 0, 1))]

    def d2d_start(self):
        self.st0 = self.comm.send(self.part.at[1 - self.core], self.r0, self.sibling)

    def rs1_start(self):
        self.st0.wait_recv()
        self.part[pl.ds(self.core, 1)] += self.r0[...][None]
        self.st = [rs_start(self.comm, self.rings[k][0], self.v1(self.part, k), self.b1(k)) for k in range(2)]

    def rs1_mid(self):
        self.st = [rs_mid(self.comm, self.rings[k][0], self.v1(self.part, k), self.b1(k), self.st[k]) for k in range(2)]

    def rs2_start(self):
        for k in range(2):
            view = self.v1(self.part, k)

            def put(half, val, view=view, k=k):
                view(self.rings[k][0].me, half)[...] = val
            rs_end(self.rings[k][0], view, self.b1(k), self.st[k], put)
            self.st[k] = rs_start(self.comm, self.rings[k][1], self.v2(self.part, k), self.b2(k))

    def rs2_mid(self):
        self.st = [rs_mid(self.comm, self.rings[k][1], self.v2(self.part, k), self.b2(k), self.st[k]) for k in range(2)]

    def ag2_start(self):
        for k in range(2):
            dst = self.v2(self.full, k)

            def put(half, val, dst=dst, k=k):
                dst(self.rings[k][1].me, half)[...] = val
            rs_end(self.rings[k][1], self.v2(self.part, k), self.b2(k), self.st[k], put)
            self.st[k] = ag_start(self.comm, self.rings[k][1], lambda b, k=k: self.full.at[self.core, k, self.rings[k][0].me, b])

    def ag2_mid(self):
        self.st = [ag_mid(self.comm, self.rings[k][1], self.v2(self.full, k), self.st[k]) for k in range(2)]

    def ag1_start(self):
        for k in range(2):
            ag_end(self.st[k])
            self.st[k] = ag_start(self.comm, self.rings[k][0], lambda a, k=k: self.full.at[self.core, k, a])

    def ag1_mid(self):
        self.st = [ag_mid(self.comm, self.rings[k][0], self.v1(self.full, k), self.st[k]) for k in range(2)]

    def d2d_back(self):
        for k in range(2):
            ag_end(self.st[k])
        half = self.full.at[self.core]
        self.st0 = self.comm.send(half, half, self.sibling)

    def finish(self):
        self.st0.wait_recv()


STEPS = ('d2d_start', 'rs1_start', 'rs1_mid', 'rs2_start', 'rs2_mid', 'ag2_start', 'ag2_mid', 'ag1_start', 'ag1_mid', 'd2d_back', 'finish')


def skew(mat, sign):
    rows = lax.broadcasted_iota(jnp.int32, mat.shape, 0)
    bit = 1
    while bit < mat.shape[0]:
        amount = bit if sign > 0 else LANES - bit
        mat = jnp.where((rows & bit) != 0, pltpu.roll(mat, amount, 1), mat)
        bit *= 2
    return mat


def kernel(n, f_ref, pred_ref, we_ref, wp_ref, wo_ref, lab_ref, flen_ref, llen_ref,
           loss_ref, genc_ref, full_out, full_pred, full_enc,
           g_ref, abuf, a_ref, act_ref, c_ref, onehot_ref, h_ref, z_ref, e_ref, bt_ref, lt_ref, rs_ref,
           sb_ref, sl_ref, al_ref, be_ref, c1_ref, gb_ref, gl_ref, dz_ref, dc_ref, dabuf, darecv, daloc, lossbuf,
           p_out, p_pred, p_enc, r0o, r1o, r2o, r0p, r1p, r2p, r0e, r1e, r2e,
           gsem, asend, arecv, dsend, drecv, ssem, rsem):
    me = lax.axis_index('seq')
    core, x, y = me % 2, (me // 2) % SIDE, me // (2 * SIDE)

    def dev(i, j, c):
        return (j * SIDE + i) * 2 + c

    n_t, n_u, n_j, n_v = a_ref.shape[0], c_ref.shape[0], c_ref.shape[1], wo_ref.shape[1]
    tl = n_t // n
    rows = BLK_T * n_u
    n_blk = n_t // BLK_T

    gcopy = pltpu.make_async_copy(pred_ref.at[me], g_ref, gsem)
    gcopy.start()
    barrier = pltpu.get_barrier_semaphore()

    def greet(p, c):
        pl.semaphore_signal(barrier, inc=1, device_id={'seq': (me + p) % n}, device_id_type=pl.DeviceIdType.MESH)
        return c
    lax.fori_loop(1, n, greet, 0)

    act_ref[...] = dot(f_ref[...], we_ref[...], 1, 0).astype(BF16).astype(F32)

    def spread(r, c):
        abuf[r] = act_ref[pl.ds(r, 1), :]
        return c
    lax.fori_loop(0, n_t, spread, 0)

    def own(k, c):
        a_ref[me * tl + k] = act_ref[pl.ds(me * tl + k, 1), :]
        return c
    lax.fori_loop(0, tl, own, 0)
    pl.semaphore_wait(barrier, n - 1)

    def a_copy(p):
        to = (me + p) % n
        return pltpu.make_async_remote_copy(src_ref=abuf.at[pl.ds(to * tl, tl)], dst_ref=a_ref.at[pl.ds(me * tl, tl)], send_sem=asend.at[p],
                                            recv_sem=arecv.at[p], device_id={'seq': to}, device_id_type=pl.DeviceIdType.MESH)

    def a_go(p, c):
        a_copy(p).start()
        return c
    lax.fori_loop(1, n, a_go, 0)

    gcopy.wait()
    c_ref[...] = dot(g_ref[...], wp_ref[...], 1, 0).astype(BF16).astype(F32)
    u_row = lax.broadcasted_iota(jnp.int32, (n_u, n_u), 0)
    u_col = lax.broadcasted_iota(jnp.int32, (n_u, n_u), 1)
    lab_row = lab_ref[pl.ds(me, 1), :].astype(F32)
    lab_col = jnp.sum(jnp.where(u_row == u_col, lab_row, 0.0), axis=1, keepdims=True)
    onehot_ref[...] = jnp.where(lax.broadcasted_iota(jnp.int32, (n_u, n_v), 1).astype(F32) == lab_col, 1.0, 0.0)
    bt_ref[...] = jnp.full_like(bt_ref, NEG)
    lt_ref[...] = jnp.full_like(lt_ref, NEG)
    rs_ref[...] = jnp.zeros_like(rs_ref)

    def a_wait(p, c):
        a_copy(p).wait_recv()
        return c
    lax.fori_loop(1, n, a_wait, 0)

    lane = lax.broadcasted_iota(jnp.int32, (n_u, LANES), 1)
    u_sub = lax.broadcasted_iota(jnp.int32, (n_u, LANES), 0)

    def fwd(i, c):
        for k in range(BLK_T):
            h_ref[pl.ds((i * BLK_T + k) * n_u, n_u), :] = jnp.tanh(a_ref[i * BLK_T + k] + c_ref[...]).astype(BF16)
        z_ref[...] = dot(h_ref[pl.ds(i * rows, rows), :], wo_ref[...], 1, 0)
        for k in range(BLK_T):
            t = i * BLK_T + k
            zt = z_ref[k * n_u:(k + 1) * n_u, :]
            m = jnp.max(zt, axis=1, keepdims=True)
            e = jnp.exp(zt - m)
            s = jnp.sum(e, axis=1, keepdims=True)
            zl = jnp.sum(zt * onehot_ref[...], axis=1, keepdims=True)
            e_ref[pl.ds(t * n_u, n_u), :] = e
            lse = m + jnp.log(s)
            here = lane == t
            bt_ref[...] = jnp.where(here, zt[:, :1] - lse, bt_ref[...])
            lt_ref[...] = jnp.where(here, zl - lse, lt_ref[...])
            rs_ref[...] = jnp.where(here, 1.0 / s, rs_ref[...])
        return c
    lax.fori_loop(0, n_blk, fwd, 0)

    fill = jnp.full((LANES - n_u, LANES), NEG, F32)
    lt = jnp.where(u_sub == n_u - 1, NEG, lt_ref[...])
    sb_ref[...] = jnp.concatenate([skew(bt_ref[...], 1), fill], axis=0).T
    sl_ref[...] = jnp.concatenate([skew(lt, 1), fill], axis=0).T

    t_len = flen_ref[me]
    u_len = llen_ref[me]
    u_id = lax.broadcasted_iota(jnp.int32, (1, LANES), 1)
    bound = jnp.where(u_id == u_len, 0.0, NEG).astype(F32)
    start = jnp.where(u_id == 0, 0.0, NEG).astype(F32)
    last = n_t + n_u - 1
    al_ref[0:1, :] = start
    be_ref[last:last + 1, :] = bound
    be_ref[last + 1:last + 9, :] = jnp.full((8, LANES), NEG, F32)

    def chain(k, carry):
        alpha, beta = carry
        d = last - 1 - k
        xa = alpha + sb_ref[pl.ds(k, 1), :]
        ya = pltpu.roll(alpha + sl_ref[pl.ds(k, 1), :], 1, 1)
        xb = beta + sb_ref[pl.ds(d, 1), :]
        yb = pltpu.roll(beta, LANES - 1, 1) + sl_ref[pl.ds(d, 1), :]
        alpha = lse2(xa, ya)
        beta = jnp.where(d - u_id >= t_len, bound, lse2(xb, yb))
        al_ref[pl.ds(k + 1, 1), :] = alpha
        be_ref[pl.ds(d, 1), :] = beta
        return alpha, beta
    _, beta0 = lax.fori_loop(0, last, chain, (start, bound))
    logp = jnp.sum(jnp.where(u_id == 0, beta0, 0.0), axis=1, keepdims=True)

    d_id = lax.broadcasted_iota(jnp.int32, (LANES, LANES), 0)
    ul_id = lax.broadcasted_iota(jnp.int32, (LANES, LANES), 1)
    t_id = d_id - ul_id
    ok = (t_id >= 0) & (t_id < t_len) & (ul_id < n_u)
    up = be_ref[1:LANES + 1, :]
    base = al_ref[...] - logp
    gb = jnp.where(ok, jnp.exp(jnp.minimum(base + sb_ref[...] + up, 0.0)), 0.0)
    gl = jnp.where(ok & (ul_id < n_u - 1), jnp.exp(jnp.minimum(base + sl_ref[...] + pltpu.roll(up, LANES - 1, 1), 0.0)), 0.0)
    gb = skew(gb.T[:n_u], -1)
    gl = skew(gl.T[:n_u], -1)
    gb_ref[...] = gb
    gl_ref[...] = gl
    c1_ref[...] = (gb + gl) * rs_ref[...]

    dc_ref[...] = jnp.zeros_like(dc_ref)
    p_out[...] = jnp.zeros_like(p_out)
    v0 = lax.broadcasted_iota(jnp.int32, (n_u, LANES), 1) == 0

    def bwd(i, c):
        turn = (LANES - i * BLK_T) % LANES
        c1 = pltpu.roll(c1_ref[...], turn, 1)
        gbr = pltpu.roll(gb_ref[...], turn, 1)
        glr = pltpu.roll(gl_ref[...], turn, 1)
        for k in range(BLK_T):
            t = i * BLK_T + k
            dz = e_ref[pl.ds(t * n_u, n_u), :] * c1[:, k:k + 1] - glr[:, k:k + 1] * onehot_ref[...]
            dz_ref[k * n_u:(k + 1) * n_u, LANES:] = dz[:, LANES:].astype(BF16)
            dz_ref[k * n_u:(k + 1) * n_u, :LANES] = (dz[:, :LANES] - jnp.where(v0, gbr[:, k:k + 1], 0.0)).astype(BF16)
        hb = h_ref[pl.ds(i * rows, rows), :]
        for q in range(n_v // 256):
            r = dot(hb, dz_ref[:, q * 256:(q + 1) * 256], 0, 0)
            p_out[2 * q * n_j:(2 * q + 1) * n_j] += r[:, :LANES]
            p_out[(2 * q + 1) * n_j:(2 * q + 2) * n_j] += r[:, LANES:]
        dh = dot(dz_ref[...], wo_ref[...], 1, 1)
        hf = hb.astype(F32)
        dp = (dh * (1.0 - hf * hf)).astype(BF16).astype(F32)
        for k in range(BLK_T):
            t = i * BLK_T + k
            dpt = dp[k * n_u:(k + 1) * n_u]
            dabuf[t // tl, t % tl] = jnp.sum(dpt, axis=0, keepdims=True).astype(BF16).astype(F32)
            dc_ref[...] += dpt
        return c
    lax.fori_loop(0, n_blk, bwd, 0)

    def put_loss(s, c):
        dabuf[s, tl] = jnp.broadcast_to(-logp, (1, n_j))
        return c
    lax.fori_loop(0, n, put_loss, 0)

    def keep(k, c):
        darecv[me, k] = dabuf[me, k]
        return c
    lax.fori_loop(0, tl + 1, keep, 0)

    def d_copy(p):
        to = (me + p) % n
        return pltpu.make_async_remote_copy(src_ref=dabuf.at[to], dst_ref=darecv.at[me], send_sem=dsend.at[p],
                                            recv_sem=drecv.at[p], device_id={'seq': to}, device_id_type=pl.DeviceIdType.MESH)

    def d_go(p, c):
        d_copy(p).start()
        return c
    lax.fori_loop(1, n, d_go, 0)

    gwp = dot(g_ref[...], dc_ref[...].astype(BF16), 0, 0)
    for q in range(n_j // LANES):
        p_pred[q * n_j:(q + 1) * n_j] = gwp[:, q * LANES:(q + 1) * LANES]
    used = n_j * n_j // LANES
    if used < p_pred.shape[0]:
        p_pred[used:] = jnp.zeros((p_pred.shape[0] - used, LANES), F32)

    def d_wait(p, c):
        d_copy(p).wait_recv()
        return c
    lax.fori_loop(1, n, d_wait, 0)

    def collect(b, c):
        for k in range(tl):
            daloc[pl.ds(b * tl + k, 1), :] = darecv[b, k]
        lossbuf[pl.ds(b, 1), :] = darecv[b, tl][:, :LANES]
        return c
    lax.fori_loop(0, n, collect, 0)
    loss_ref[...] = lossbuf[...]
    dal = daloc[...].astype(BF16)
    genc_ref[...] = dot(dal, we_ref[...], 1, 1).astype(BF16)
    gwe = dot(f_ref[...], dal, 0, 0)
    n_e = f_ref.shape[1]
    for q in range(n_j // LANES):
        p_enc[q * n_e:(q + 1) * n_e] = gwe[:, q * LANES:(q + 1) * LANES]

    comm = Comm(ssem, rsem)
    pos = (core, x, y, dev)

    def six(ref, m):
        return ref.reshape(2, 2, SIDE, SIDE, m, LANES)
    ars = [AllReduce(comm, pos, six(p, p.shape[0] // 64), full, a, b, c) for p, full, a, b, c in
           ((p_out, full_out, r0o, r1o, r2o), (p_pred, full_pred, r0p, r1p, r2p), (p_enc, full_enc, r0e, r1e, r2e))]
    for step in STEPS:
        for ar in ars:
            getattr(ar, step)()

    def sends_done(p, c):
        a_copy(p).wait_send()
        d_copy(p).wait_send()
        return c
    lax.fori_loop(1, n, sends_done, 0)
    comm.drain()


def solution(mesh):
    n = mesh.shape['seq']
    assert n == 2 * SIDE * SIDE
    parts = 2 * n

    def local_fn(enc_out, pred_out, w_enc, w_pred, w_out, labels, frame_len, label_len):
        n_utt, n_loc, n_e = enc_out.shape
        _, n_u, n_g = pred_out.shape
        n_j, n_v = w_out.shape
        n_t = n_loc * n
        assert n_utt == n
        lab_ids = jnp.concatenate([labels, jnp.full((n_utt, 1), -1, jnp.int32)], axis=1)
        m_out, m_pred, m_enc = (pieces_rows(r, c, parts) for r, c in ((n_j, n_v), (n_g, n_j), (n_e, n_j)))
        vm = pl.BlockSpec(memory_space=pltpu.VMEM)
        sm = pl.BlockSpec(memory_space=pltpu.SMEM)

        def six(m):
            return (2, 2, SIDE, SIDE, m, LANES)

        def ar_scratch(m):
            return [pltpu.VMEM((2, SIDE, SIDE, m, LANES), F32), pltpu.VMEM((2, 6, 2, m, LANES), F32), pltpu.VMEM((2, 6, m, LANES), F32)]
        sq = pltpu.VMEM((LANES, LANES), F32)
        hf = pltpu.VMEM((n_u, LANES), F32)
        n_sem = 3 * 42
        outs = pl.pallas_call(
            functools.partial(kernel, n),
            out_shape=(jax.ShapeDtypeStruct((n, LANES), F32), jax.ShapeDtypeStruct((n_utt * n_loc, n_e), BF16),
                       jax.ShapeDtypeStruct(six(m_out), F32), jax.ShapeDtypeStruct(six(m_pred), F32), jax.ShapeDtypeStruct(six(m_enc), F32)),
            in_specs=[vm, pl.BlockSpec(memory_space=pl.ANY), vm, vm, vm, vm, sm, sm],
            out_specs=(vm,) * 5,
            scratch_shapes=[
                pltpu.VMEM((n_u, n_g), BF16), pltpu.VMEM((n_t, 1, n_j), F32), pltpu.VMEM((n_t, 1, n_j), F32), pltpu.VMEM((n_t, n_j), F32),
                pltpu.VMEM((n_u, n_j), F32), pltpu.VMEM((n_u, n_v), F32), pltpu.VMEM((n_t * n_u, n_j), BF16), pltpu.VMEM((BLK_T * n_u, n_v), F32),
                pltpu.VMEM((n_t * n_u, n_v), F32), hf, hf, hf,
                sq, sq, sq, pltpu.VMEM((LANES + 8, LANES), F32), hf, hf, hf, pltpu.VMEM((BLK_T * n_u, n_v), BF16), pltpu.VMEM((n_u, n_j), F32),
                pltpu.VMEM((n, n_loc + 1, 1, n_j), F32), pltpu.VMEM((n, n_loc + 1, 1, n_j), F32), pltpu.VMEM((n_t, n_j), F32), pltpu.VMEM((n, LANES), F32),
                pltpu.VMEM((parts * m_out, LANES), F32), pltpu.VMEM((parts * m_pred, LANES), F32), pltpu.VMEM((parts * m_enc, LANES), F32),
                *ar_scratch(m_out), *ar_scratch(m_pred), *ar_scratch(m_enc),
                pltpu.SemaphoreType.DMA, pltpu.SemaphoreType.DMA((n,)), pltpu.SemaphoreType.DMA((n,)), pltpu.SemaphoreType.DMA((n,)), pltpu.SemaphoreType.DMA((n,)),
                pltpu.SemaphoreType.DMA((n_sem,)), pltpu.SemaphoreType.DMA((n_sem,))],
            compiler_params=pltpu.CompilerParams(collective_id=0, has_side_effects=True, vmem_limit_bytes=62 * 1024 * 1024),
        )(enc_out.reshape(n_utt * n_loc, n_e), pred_out, w_enc, w_pred, w_out, lab_ids, frame_len, label_len)
        loss, genc, fo, fp, fe = outs

        def unflat(full, r, c):
            return full.reshape(-1, LANES)[:r * c // LANES].reshape(c // LANES, r, LANES).transpose(1, 0, 2).reshape(r, c)
        return (loss[:, 0], genc.reshape(n_utt, n_loc, n_e), unflat(fe, n_e, n_j), unflat(fp, n_g, n_j), unflat(fo, n_j, n_v))

    in_specs = (P('dp', 'seq', None), P('dp', None, None), P(None, None), P(None, None), P(None, None), P('dp', None), P('dp'), P('dp'))
    out_specs = (P('dp'), P('dp', 'seq', None), P('dp', None), P('dp', None), P('dp', None))
    return jax.shard_map(local_fn, mesh=mesh, in_specs=in_specs, out_specs=out_specs, check_vma=False)
```

time: 1300 us -> 144 us (0.11)
  other arithmetic: 541 us -> 0 us
  waiting for transfers between devices: 293 us -> 0 us
  starting transfers between devices: 234 us -> 0 us
  Pallas kernels: 0 us -> 125 us
  matrix products: 77.4 us -> 0 us
  blocking collectives: 67.1 us -> 0 us
  local copies, waits for them, and re-layouts: 58.1 us -> 18.4 us
  between operations: 14.8 us -> 0.66 us
    another operation x256 -> x0, other arithmetic: 461 us -> none  [the longest x64 345 us: frame_step(): lax.cumlogsumexp(next_row + frame_blank + lab_sum, axis=1, reverse=True)]
    ppermute x62 -> x0, starting transfers between devices: 234 us -> none  [the longest x31 173 us: alpha_hop(): received = lax.ppermute(x_out, 'seq', fwd_pairs)]
    ppermute x62 -> x0, waiting for transfers between devices: 190 us -> none  [the longest x31 164 us: beta_hop(): received = lax.ppermute(first_row, 'seq', bwd_pairs)]
    pallas_call x0 -> x1, Pallas kernels: none -> 125 us  [local_fn(): pl.pallas_call(functools.partial(kernel, n), out_shape=(jax.ShapeDtypeStr...]
    psum x1 -> x0, waiting for transfers between devices: 102 us -> none  [local_fn(): gw_enc, gw_pred, gw_out = lax.psum((gw_enc, gw_pred, gw_out), 'seq')]
    dot_general x10 -> x0, matrix products: 77.4 us -> none  [the longest x1 20.9 us: joint_lattice(): jnp.einsum('btuj,buj->btu', hidden, lab_w, preferred_element_type=jnp.flo...]
    psum x1 -> x0, blocking collectives: 67.1 us -> none  [local_fn(): log_prob = lax.psum(jnp.where(seq_idx == 0, first_row[:, 0], 0.0), 'seq')]
    ge x64 -> x0, other arithmetic: 41.5 us -> none  [frame_step(): beta_row = jnp.where((frame_id >= frame_len)[:, None], boundary, beta_row)]
  transfers between devices with their start and end apart: 63 -> 0, of which waited for: 63 -> 0; matrix products, arithmetic and copies ran while one was open for 0% -> 0% of each run, Pallas kernels for 0% -> 0%
where the time goes in v1:
time: 144 us
  Pallas kernels  125 us (87%)
  local copies, waits for them, and re-layouts  18.4 us (13%)
    pallas_call x1, Pallas kernels, local_fn(): pl.pallas_call(functools.partial(kernel, n), out_shape=(jax.ShapeDtypeStr...  125 us
    unnamed x2, local copies, waits for them, and re-layouts  3.78 us
    reshape x1, local copies, waits for them, and re-layouts, unflat(): full.reshape(-1, LANES)[:r * c // LANES].reshape(c // LANES, r, LANES)  3.59 us

profile of v1, /device:TPU:97, one launch (start us, length us, event | category | flops | bytes accessed | tf_op | source)
XLA Modules:
  0.0 144.1 jit_solution(11531417132109982383)
XLA Ops:
  0.6 1.3 concatenate.3.lab_ref
  2.0 1.6 %reshape.31.f_ref = bf16[64,1024]{1,0:T(8,128)(2,1)} reshape(bf16[32,2,1024]{2,1,0:T(2,128)(2,1)} %param.8) | data formatting | bytes 262144 | tf_op jit(solution)/shard_map/reshape | solution.py:459
  3.6 125.0 %shard_map.119 = (f32[32,128]{1,0:T(8,128)}, bf16[64,1024]{1,0:T(8,128)(2,1)}, f32[2,2,4,4,80,128]{5,4,3,2,1,0:T(8,128)}, f32[2,2,4,4,56,128]{5,4,3,2,1,0:T(8,128)}, f32[2,2,4,4,80,128]{5,4,3,2,1,0:T(8,128)}) custom-call(bf16[64,1024]{1,0:T(8,128)(2,1)} %reshape.31.f_ref, bf16[32,64,640]{2,1,0:T(8,128)(2,1)} %pred_ref.1, bf16[1024,640]{1,0:T(8,128)(2,1)} %we_ref.1, ...), custom_call_target="tpu_custom_call" | custom-call | tf_op jit(solution)/shard_map/pallas_call | solution.py:442
  128.6 1.3 slice_reduce_fusion
  129.9 1.6 %reshape.32 = bf16[32,2,1024]{2,1,0:T(2,128)(2,1)} reshape(bf16[64,1024]{1,0:T(8,128)(2,1)} %get-tuple-element.11) | data formatting | bytes 262144 | tf_op jit(solution)/shard_map/reshape | solution.py:464
  131.5 1.5 %slice.8 = f32[3200,128]{1,0:T(8,128)S(1)} slice(f32[3584,128]{1,0:T(8,128)} %bitcast.22), slice={[0:3200], [0:128]} | slice | bytes 3276800 | tf_op jit(solution)/shard_map/slice | solution.py:463
  133.1 1.4 %copy.21 = f32[640,5,128]{0,2,1:T(8,128)S(1)} copy(f32[640,5,128]{2,0,1:T(8,128)S(1)} %bitcast.17) | data formatting | bytes 3276800 | tf_op jit(solution)/shard_map/transpose | solution.py:463
  134.5 1.7 %copy.24 = f32[640,640]{1,0:T(8,128)} copy(f32[640,640]{0,1:T(8,128)S(1)} %bitcast.18) | data formatting | bytes 3276800
  136.2 2.2 %copy.20 = f32[5,1024,128]{1,2,0:T(8,128)S(1)} copy(f32[5,1024,128]{2,1,0:T(8,128)} %bitcast.20) | data formatting | bytes 5242880 | tf_op jit(solution)/shard_map/reshape;reshape | solution.py:463
  138.4 2.1 %copy.23 = f32[1024,640]{1,0:T(8,128)} copy(f32[1024,640]{0,1:T(8,128)S(1)} %bitcast.16) | data formatting | bytes 5242880
  140.5 3.6 %copy.27 = f32[8,80,8,128]{3,2,0,1:T(8,128)} copy(f32[8,80,8,128]{3,2,1,0:T(8,128)} %bitcast.19) | data formatting | bytes 5242880 | tf_op jit(solution)/shard_map/reshape | solution.py:463

commit v2 on v1

v2 whole, which is shorter than its diff:
```python
import functools

import jax
import jax.numpy as jnp
from jax import lax
from jax.experimental import pallas as pl
from jax.experimental.pallas import tpu as pltpu
from jax.sharding import PartitionSpec as P

NEG = -1.0e30
SIDE = 4
LANES = 128
BLK_T = 8
F32 = jnp.float32
BF16 = jnp.bfloat16


def dot(a, b, ca, cb):
    return lax.dot_general(a, b, (((ca,), (cb,)), ((), ())), preferred_element_type=F32)


def lse2(x, y):
    m = jnp.maximum(x, y)
    return m + jnp.log(1.0 + jnp.exp(-jnp.abs(x - y)))


def pieces_rows(rows, cols, parts):
    tiles = rows * cols // (8 * LANES)
    return -(-tiles // parts) * 8


class Comm:
    def __init__(self, send_sem, recv_sem):
        self.send_sem, self.recv_sem, self.used, self.sent = send_sem, recv_sem, 0, {}

    def send(self, src, dst, dev):
        k, slot = self.used, self.used % self.send_sem.shape[0]
        self.used += 1
        if slot in self.sent:
            self.sent.pop(slot).wait_send()
        cp = pltpu.make_async_remote_copy(src_ref=src, dst_ref=dst, send_sem=self.send_sem.at[slot], recv_sem=self.recv_sem.at[k],
                                          device_id={'seq': dev}, device_id_type=pl.DeviceIdType.MESH)
        cp.start()
        self.sent[slot] = cp
        return cp

    def drain(self):
        for cp in self.sent.values():
            cp.wait_send()
        self.sent = {}


class Ring:
    def __init__(self, pos, dev_of):
        self.me, self.r, self.l, self.o = pos, (pos + 1) % SIDE, (pos + 3) % SIDE, (pos + 2) % SIDE
        self.right, self.left, self.opp = dev_of(self.r), dev_of(self.l), dev_of(self.o)


def rs_start(comm, ring, view, buf):
    return (comm.send(view(ring.o, 0), buf[0], ring.right), comm.send(view(ring.o, 1), buf[2], ring.left),
            comm.send(view(ring.r, 1), buf[1], ring.right), comm.send(view(ring.l, 0), buf[3], ring.left))


def rs_mid(comm, ring, view, buf, st):
    st[0].wait_recv()
    v = view(ring.r, 0)
    v[...] += buf[0][...]
    a = comm.send(v, buf[4], ring.right)
    st[1].wait_recv()
    v = view(ring.l, 1)
    v[...] += buf[2][...]
    b = comm.send(v, buf[5], ring.left)
    return st + (a, b)


def rs_end(ring, view, buf, st, out):
    for k in (2, 3, 4, 5):
        st[k].wait_recv()
    out(0, view(ring.me, 0)[...] + buf[4][...] + buf[3][...])
    out(1, view(ring.me, 1)[...] + buf[5][...] + buf[1][...])


def ex_start(comm, ring, view, buf):
    return tuple(comm.send(view(at), b, to) for at, b, to in zip((ring.r, ring.l, ring.o), buf, (ring.right, ring.left, ring.opp)))


def ag_start(comm, ring, whole):
    v = whole(ring.me)
    return (comm.send(v, v, ring.right), comm.send(v, v, ring.left))


def ag_mid(comm, ring, half, st):
    st[0].wait_recv()
    v = half(ring.l, 0)
    a = comm.send(v, v, ring.right)
    st[1].wait_recv()
    v = half(ring.r, 1)
    b = comm.send(v, v, ring.left)
    return (a, b)


def ag_end(st):
    st[0].wait_recv()
    st[1].wait_recv()


class AllReduce:
    def __init__(self, comm, pos, full, part=None, r0=None, r1=None, r2=None):
        self.comm, (self.core, x, y, dev) = comm, pos
        self.part, self.full, self.r0, self.r1, self.r2 = part, full, r0, r1, r2
        rx = Ring(x, lambda i: dev(i, y, self.core))
        ry = Ring(y, lambda i: dev(x, i, self.core))
        self.rings = ((rx, ry), (ry, rx))
        self.sibling = dev(x, y, 1 - self.core)

    def v1(self, ref, k):
        return lambda a, half: ref.at[self.core, k, a, pl.ds(2 * half, 2)]

    def v2(self, ref, k):
        return lambda b: ref.at[self.core, k, self.rings[k][0].me, b]

    def b1(self, k):
        return [self.r1.at[k, s] for s in range(6)]

    def b2(self, k):
        return [self.r2.at[k, s] for s in range(3)]

    def d2d_start(self):
        self.st0 = self.comm.send(self.part.at[1 - self.core], self.r0, self.sibling)

    def rs1_start(self):
        self.st0.wait_recv()
        self.part[pl.ds(self.core, 1)] += self.r0[...][None]
        self.st = [rs_start(self.comm, self.rings[k][0], self.v1(self.part, k), self.b1(k)) for k in range(2)]

    def rs1_mid(self):
        self.st = [rs_mid(self.comm, self.rings[k][0], self.v1(self.part, k), self.b1(k), self.st[k]) for k in range(2)]

    def rs2_start(self):
        for k in range(2):
            view = self.v1(self.part, k)

            def put(half, val, view=view, k=k):
                view(self.rings[k][0].me, half)[...] = val
            rs_end(self.rings[k][0], view, self.b1(k), self.st[k], put)
            self.st[k] = ex_start(self.comm, self.rings[k][1], self.v2(self.part, k), self.b2(k))

    def mine(self, k):
        return self.full.at[self.core, k, self.rings[k][0].me, self.rings[k][1].me]

    def gather_start(self):
        self.st = []
        for k in range(2):
            own = self.mine(k)
            self.st.append(ex_start(self.comm, self.rings[k][1], lambda b, own=own: own, (own, own, own)))

    def ag2_start(self):
        for k in range(2):
            for cp in self.st[k]:
                cp.wait_recv()
            got = self.b2(k)
            self.mine(k)[...] = self.v2(self.part, k)(self.rings[k][1].me)[...] + got[0][...] + got[1][...] + got[2][...]
        self.gather_start()

    def ag1_start(self):
        for k in range(2):
            for cp in self.st[k]:
                cp.wait_recv()
            self.st[k] = ag_start(self.comm, self.rings[k][0], lambda a, k=k: self.full.at[self.core, k, a])

    def ag1_mid(self):
        self.st = [ag_mid(self.comm, self.rings[k][0], self.v1(self.full, k), self.st[k]) for k in range(2)]

    def d2d_back(self):
        for k in range(2):
            ag_end(self.st[k])
        half = self.full.at[self.core]
        self.st0 = self.comm.send(half, half, self.sibling)

    def finish(self):
        self.st0.wait_recv()


def skew(mat):
    return pltpu.roll(mat, 0, 1, stride=1, stride_axis=0)


def unskew(mat):
    rows = lax.broadcasted_iota(jnp.int32, mat.shape, 0)
    bit = 1
    while bit < mat.shape[0]:
        mat = jnp.where((rows & bit) != 0, pltpu.roll(mat, LANES - bit, 1), mat)
        bit *= 2
    return mat


def lse(terms):
    m = functools.reduce(jnp.maximum, terms)
    return m + jnp.log(functools.reduce(jnp.add, [jnp.exp(x - m) for x in terms]))


def shift(x, k):
    return x if k == 0 else pltpu.roll(x, k % LANES, 1)


def compose(first, second):
    r = len(first) - 1
    return [lse([shift(first[k - j], j) + second[j] for j in range(max(0, k - r), min(r, k) + 1)]) for k in range(2 * r + 1)]


def every(ref, k, start, step):
    return ref[k, pl.ds(start, LANES // step, stride=step), :]


def lattice(w_refs, al_ref, be_ref, start, bound, levels):
    for lv in range(levels):
        src, dst, rows = w_refs[lv], w_refs[lv + 1], LANES >> lv
        r = 2 ** lv
        first = [src[k, pl.ds(0, rows // 2, stride=2), :] for k in range(r + 1)]
        second = [src[k, pl.ds(1, rows // 2, stride=2), :] for k in range(r + 1)]
        for k, w in enumerate(compose(first, second)):
            dst[k, :rows // 2, :] = w
    hop = 2 ** levels
    top, n_hop = w_refs[levels], LANES // hop
    al_ref[0:1, :] = start
    be_ref[LANES:LANES + 8, :] = jnp.broadcast_to(bound, (8, LANES))

    def chain(i, carry):
        alpha, beta = carry
        j = n_hop - 1 - i
        alpha = lse([shift(alpha, k) + top[k, pl.ds(i, 1), :] for k in range(hop + 1)])
        beta = lse([shift(beta + top[k, pl.ds(j, 1), :], -k) for k in range(hop + 1)])
        al_ref[pl.ds((i + 1) * hop, 1), :] = alpha
        be_ref[pl.ds(j * hop, 1), :] = beta
        return alpha, beta
    lax.fori_loop(0, n_hop, chain, (start, bound))
    for lv in range(levels - 1, -1, -1):
        r = 2 ** lv
        n_r = LANES // (2 * r)
        al = al_ref[pl.ds(0, n_r, stride=2 * r), :]
        be = be_ref[pl.ds(2 * r, n_r, stride=2 * r), :]
        al_ref[pl.ds(r, n_r, stride=2 * r), :] = lse([shift(al, k) + w_refs[lv][k, pl.ds(0, n_r, stride=2), :] for k in range(r + 1)])
        be_ref[pl.ds(r, n_r, stride=2 * r), :] = lse([shift(be + w_refs[lv][k, pl.ds(1, n_r, stride=2), :], -k) for k in range(r + 1)])


LEVELS = 3


def kernel(n, f_hbm, pred_ref, we_hbm, wp_hbm, wo_hbm, lab_ref, flen_ref, llen_ref,
           loss_out, genc_out, gwe_out, gwp_out, gwo_out,
           f_ref, we_ref, wp_ref, wo_ref, g_ref, abuf, a_ref, act_ref, c_ref, onehot_ref, h_ref, z0_ref, z1_ref, e_ref, bt_ref, lt_ref, rs_ref,
           w0, w1, w2, w3, al_ref, be_ref, c1_ref, gb_ref, gl_ref, dz0_ref, dz1_ref, dc_ref, dabuf, darecv, daloc, loss_col, lossbuf, genc_ref,
           fg_ref, dg_ref, p_out, p_pred, s_out, s_pred, r0a, r1a, r2a, r0b, r1b, r2b, r0p, r1p, r2p,
           insem, outsem, asend, arecv, dsend, drecv, ssem, rsem):
    me = lax.axis_index('seq')
    core, x, y = me % 2, (me // 2) % SIDE, me // (2 * SIDE)

    def dev(i, j, c):
        return (j * SIDE + i) * 2 + c

    n_t, n_u, n_j, n_v = n * a_ref.shape[1], c_ref.shape[0], c_ref.shape[1], wo_ref.shape[1]
    n_e = f_ref.shape[2]
    tl = n_t // n
    rows = BLK_T * n_u
    n_blk = n_t // BLK_T
    n_h = n_v // 2

    barrier = pltpu.get_barrier_semaphore()

    def greet(p, c):
        pl.semaphore_signal(barrier, inc=1, device_id={'seq': (me + p) % n}, device_id_type=pl.DeviceIdType.MESH)
        return c
    lax.fori_loop(1, n, greet, 0)
    loads = [pltpu.make_async_copy(src, dst, insem.at[k]) for k, (src, dst) in enumerate(
        ((f_hbm, f_ref), (we_hbm, we_ref), (pred_ref.at[me], g_ref), (wp_hbm, wp_ref), (wo_hbm, wo_ref)))]
    for cp in loads:
        cp.start()
    comm = Comm(ssem, rsem)
    pos = (core, x, y, dev)

    def six(ref, base, m):
        return ref.at[pl.ds(base, 64 * m)].reshape(2, 2, SIDE, SIDE, m, LANES)
    m_o, m_p = n_j * n_h // LANES // 64, p_pred.shape[0] // 64
    ar0 = AllReduce(comm, pos, six(s_out, 0, m_o), six(p_out, 0, m_o), r0a, r1a, r2a)
    ar1 = AllReduce(comm, pos, six(s_out, 64 * m_o, m_o), six(p_out, 64 * m_o, m_o), r0b, r1b, r2b)
    arp = AllReduce(comm, pos, six(s_pred, 0, m_p), six(p_pred, 0, m_p), r0p, r1p, r2p)
    agf = AllReduce(comm, pos, fg_ref)
    agd = AllReduce(comm, pos, dg_ref)

    loads[0].wait()
    loads[1].wait()
    for k in range(tl):
        agf.mine(k)[...] = f_ref[:, k, :]
    f_loc = jnp.concatenate([agf.mine(k)[...] for k in range(tl)], axis=0)
    act_ref[...] = dot(f_loc, we_ref[...], 1, 0).astype(BF16).astype(F32)

    def spread(b, c):
        for k in range(tl):
            abuf[b, k] = act_ref[pl.ds(k * n + b, 1), :]
        return c
    lax.fori_loop(0, n, spread, 0)
    for k in range(tl):
        a_ref[me, k] = act_ref[pl.ds(k * n + me, 1), :]
    pl.semaphore_wait(barrier, n - 1)

    def a_copy(p):
        to = (me + p) % n
        return pltpu.make_async_remote_copy(src_ref=abuf.at[to], dst_ref=a_ref.at[me], send_sem=asend, recv_sem=arecv, device_id={'seq': to}, device_id_type=pl.DeviceIdType.MESH)

    def a_go(p, c):
        a_copy(p).start()
        return c
    lax.fori_loop(1, n, a_go, 0)
    agf.gather_start()

    loads[2].wait()
    loads[3].wait()
    c_ref[...] = dot(g_ref[...], wp_ref[...], 1, 0).astype(BF16).astype(F32)
    n_lab = lab_ref.shape[1]
    u_row = lax.broadcasted_iota(jnp.int32, (n_u, n_lab), 0)
    u_col = lax.broadcasted_iota(jnp.int32, (n_u, n_lab), 1)
    lab_row = lab_ref[pl.ds(me, 1), :].astype(F32)
    lab_col = jnp.sum(jnp.where(u_row == u_col, lab_row, 0.0), axis=1, keepdims=True)
    lab_col = jnp.where(lax.broadcasted_iota(jnp.int32, (n_u, 1), 0) < n_lab, lab_col, -1.0)
    onehot_ref[...] = jnp.where(lax.broadcasted_iota(jnp.int32, (n_u, n_v), 1).astype(F32) == lab_col, 1.0, 0.0)
    bt_ref[...] = jnp.full_like(bt_ref, NEG)
    lt_ref[...] = jnp.full_like(lt_ref, NEG)
    rs_ref[...] = jnp.zeros_like(rs_ref)
    loads[4].wait()

    others = pl.ds(0, n - 1)
    pltpu.make_async_copy(abuf.at[others], a_ref.at[others], arecv).wait()

    lane = lax.broadcasted_iota(jnp.int32, (n_u, LANES), 1)
    u_sub = lax.broadcasted_iota(jnp.int32, (n_u, LANES), 0)

    def scores(i, z_ref):
        for k in range(BLK_T):
            h_ref[pl.ds((i * BLK_T + k) * n_u, n_u), :] = jnp.tanh(a_ref[(i * BLK_T + k) // tl, (i * BLK_T + k) % tl] + c_ref[...]).astype(BF16)
        z_ref[...] = dot(h_ref[pl.ds(i * rows, rows), :], wo_ref[...], 1, 0)

    def stats(i, z_ref):
        for k in range(BLK_T):
            t = i * BLK_T + k
            zt = z_ref[k * n_u:(k + 1) * n_u, :]
            m = jnp.max(zt, axis=1, keepdims=True)
            e = jnp.exp(zt - m)
            s = jnp.sum(e, axis=1, keepdims=True)
            zl = jnp.sum(zt * onehot_ref[...], axis=1, keepdims=True)
            e_ref[pl.ds(t * n_u, n_u), :] = e
            norm = m + jnp.log(s)
            here = lane == t
            bt_ref[...] = jnp.where(here, zt[:, :1] - norm, bt_ref[...])
            lt_ref[...] = jnp.where(here, zl - norm, lt_ref[...])
            rs_ref[...] = jnp.where(here, 1.0 / s, rs_ref[...])

    def pair(i, c):
        scores(2 * i + 1, z1_ref)
        stats(2 * i, z0_ref)
        scores(2 * i + 2, z0_ref)
        stats(2 * i + 1, z1_ref)
        return c
    scores(0, z0_ref)
    n_pair = n_blk // 2 - 1
    lax.fori_loop(0, 1, pair, 0)
    agf.ag1_start()
    lax.fori_loop(1, n_pair, pair, 0)
    scores(n_blk - 1, z1_ref)
    stats(n_blk - 2, z0_ref)
    stats(n_blk - 1, z1_ref)
    agf.ag1_mid()

    t_len = flen_ref[me]
    u_len = llen_ref[me]
    fill = jnp.full((LANES - n_u, LANES), NEG, F32)
    lt = jnp.where(u_sub == n_u - 1, NEG, lt_ref[...])
    d_id = lax.broadcasted_iota(jnp.int32, (LANES, LANES), 0)
    u_id = lax.broadcasted_iota(jnp.int32, (LANES, LANES), 1)
    t_id = d_id - u_id
    past = t_id >= t_len
    sb = jnp.concatenate([skew(bt_ref[...]), fill], axis=0).T
    sl = jnp.concatenate([skew(lt), fill], axis=0).T
    sb = jnp.where(past, jnp.where(u_id == u_len, 0.0, NEG), jnp.where(t_id < 0, NEG, sb))
    sl = jnp.where(past | (t_id < 0), NEG, sl)
    w0[0] = sb
    w0[1] = pltpu.roll(sl, 1, 1)
    row_id = lax.broadcasted_iota(jnp.int32, (1, LANES), 1)
    bound = jnp.where(row_id == u_len, 0.0, NEG).astype(F32)
    start = jnp.where(row_id == 0, 0.0, NEG).astype(F32)
    lattice((w0, w1, w2, w3), al_ref, be_ref, start, bound, LEVELS)
    logp = jnp.sum(jnp.where(row_id == 0, be_ref[0:1, :], 0.0), axis=1, keepdims=True)
    ok = (t_id >= 0) & jnp.logical_not(past) & (u_id < n_u)
    up = be_ref[1:LANES + 1, :]
    base = al_ref[:LANES, :] - logp
    gb = jnp.where(ok, jnp.exp(jnp.minimum(base + w0[0] + up, 0.0)), 0.0)
    gl = jnp.where(ok & (u_id < n_u - 1), jnp.exp(jnp.minimum(base + pltpu.roll(w0[1] + up, LANES - 1, 1), 0.0)), 0.0)
    gb = unskew(gb.T[:n_u])
    gl = unskew(gl.T[:n_u])
    gb_ref[...] = gb
    gl_ref[...] = gl
    c1_ref[...] = (gb + gl) * rs_ref[...]

    for b in range(n):
        dabuf[b, tl] = jnp.broadcast_to(-logp, (1, n_j))
    dc_ref[...] = jnp.zeros_like(dc_ref)
    p_out[...] = jnp.zeros_like(p_out)
    v0 = lax.broadcasted_iota(jnp.int32, (n_u, LANES), 1) == 0

    def grad_logits(i, lo, dz_ref):
        turn = (LANES - i * BLK_T) % LANES
        c1 = pltpu.roll(c1_ref[...], turn, 1)
        gbr = pltpu.roll(gb_ref[...], turn, 1)
        glr = pltpu.roll(gl_ref[...], turn, 1)
        for k in range(BLK_T):
            at = (i * BLK_T + k) * n_u
            dz = e_ref[pl.ds(at, n_u), lo:lo + n_h] * c1[:, k:k + 1] - glr[:, k:k + 1] * onehot_ref[:, lo:lo + n_h]
            if lo == 0:
                dz_ref[pl.ds(at, n_u), LANES:] = dz[:, LANES:].astype(BF16)
                dz_ref[pl.ds(at, n_u), :LANES] = (dz[:, :LANES] - jnp.where(v0, gbr[:, k:k + 1], 0.0)).astype(BF16)
            else:
                dz_ref[pl.ds(at, n_u), :] = dz.astype(BF16)

    def grad_out(i, q0, dz_ref):
        hb = h_ref[pl.ds(i * 2 * rows, 2 * rows), :]
        r = dot(hb, dz_ref[pl.ds(i * 2 * rows, 2 * rows), :], 0, 0)
        for q in range(n_h // LANES):
            p_out[(q0 + q) * n_j:(q0 + q + 1) * n_j] += r[:, q * LANES:(q + 1) * LANES]

    def phase0(i, c):
        grad_logits(i, 0, dz0_ref)
        return c

    def phase1(i, c):
        grad_out(i, 0, dz0_ref)
        grad_logits(2 * i, n_h, dz1_ref)
        grad_logits(2 * i + 1, n_h, dz1_ref)
        return c

    def phase2(i, c):
        grad_out(i, n_h // LANES, dz1_ref)
        return c

    def grad_hidden(i, z_ref):
        at = pl.ds(i * rows, rows)
        z_ref[:, :n_j] = dot(dz0_ref[at, :], wo_ref[:, :n_h], 1, 1) + dot(dz1_ref[at, :], wo_ref[:, n_h:], 1, 1)

    def grad_pre(i, z_ref):
        for k in range(BLK_T):
            t = i * BLK_T + k
            hf = h_ref[pl.ds(t * n_u, n_u), :].astype(F32)
            dpt = (z_ref[k * n_u:(k + 1) * n_u, :n_j] * (1.0 - hf * hf)).astype(BF16).astype(F32)
            dabuf[t // tl, t % tl] = jnp.sum(dpt, axis=0, keepdims=True).astype(BF16).astype(F32)
            dc_ref[...] += dpt

    def phase3(i, c):
        grad_hidden(2 * i + 1, z1_ref)
        grad_pre(2 * i, z0_ref)
        grad_hidden(2 * i + 2, z0_ref)
        grad_pre(2 * i + 1, z1_ref)
        return c

    lax.fori_loop(0, n_blk, phase0, 0)
    agf.d2d_back()
    lax.fori_loop(0, n_blk // 2, phase1, 0)
    ar0.d2d_start()
    lax.fori_loop(0, n_blk // 4, phase2, 0)
    ar0.rs1_start()
    lax.fori_loop(n_blk // 4, n_blk // 2, phase2, 0)
    ar1.d2d_start()
    grad_hidden(0, z0_ref)
    lax.fori_loop(0, 1, phase3, 0)
    ar1.rs1_start()
    ar0.rs1_mid()
    lax.fori_loop(1, 2, phase3, 0)
    ar1.rs1_mid()
    lax.fori_loop(2, n_pair, phase3, 0)
    ar0.rs2_start()
    grad_hidden(n_blk - 1, z1_ref)
    grad_pre(n_blk - 2, z0_ref)
    grad_pre(n_blk - 1, z1_ref)

    def keep(k, c):
        darecv[me, k] = dabuf[me, k]
        return c
    lax.fori_loop(0, tl + 1, keep, 0)

    def d_copy(p):
        to = (me + p) % n
        return pltpu.make_async_remote_copy(src_ref=dabuf.at[to], dst_ref=darecv.at[me], send_sem=dsend, recv_sem=drecv, device_id={'seq': to}, device_id_type=pl.DeviceIdType.MESH)

    def d_go(p, c):
        d_copy(p).start()
        return c
    lax.fori_loop(1, n, d_go, 0)

    gwp = dot(g_ref[...], dc_ref[...].astype(BF16), 0, 0)
    for q in range(n_j // LANES):
        p_pred[q * n_j:(q + 1) * n_j] = gwp[:, q * LANES:(q + 1) * LANES]
    used = n_j * n_j // LANES
    if used < p_pred.shape[0]:
        p_pred[used:] = jnp.zeros((p_pred.shape[0] - used, LANES), F32)
    arp.d2d_start()
    ar1.rs2_start()
    ar0.ag2_start()
    arp.rs1_start()
    ar1.ag2_start()
    pltpu.make_async_copy(dabuf.at[others], darecv.at[others], drecv).wait()

    def collect(b, c):
        for k in range(tl):
            daloc[pl.ds(k * n + b, 1), :] = darecv[b, k]
        loss_col[pl.ds(b, 1), :] = darecv[b, tl][:, :n]
        return c
    lax.fori_loop(0, n, collect, 0)
    dal = daloc[...].astype(BF16)
    for k in range(2):
        agd.mine(k)[...] = dal[k * n:(k + 1) * n, :]
    agd.gather_start()
    ar0.ag1_start()
    arp.rs1_mid()
    diag = lax.broadcasted_iota(jnp.int32, (n, n), 0) == lax.broadcasted_iota(jnp.int32, (n, n), 1)
    lossbuf[...] = jnp.sum(jnp.where(diag, loss_col[...], 0.0), axis=0, keepdims=True)
    genc = dot(dal, we_ref[...], 1, 1).astype(BF16)
    for k in range(tl):
        genc_ref[:, k, :] = genc[k * n:(k + 1) * n, :]
    flush = []

    def put(src, dst):
        cp = pltpu.make_async_copy(src, dst, outsem.at[len(flush)])
        cp.start()
        flush.append(cp)
    put(lossbuf, loss_out)
    put(genc_ref, genc_out)
    agd.ag1_start()
    ar0.ag1_mid()
    ar1.ag1_start()
    arp.rs2_start()
    agd.ag1_mid()
    ar1.ag1_mid()
    arp.ag2_start()
    ar0.d2d_back()
    agd.d2d_back()
    ar1.d2d_back()
    arp.ag1_start()
    agf.finish()
    agd.finish()

    at_o, at_e, at_p = 0, n_j, n_j + n_e
    blk = n_e // 4

    def enc_block(i, c):
        fb = fg_ref[:, :, :, :, :, pl.ds(pl.multiple_of(i * blk, blk), blk)].reshape(n * n_t, blk)
        e_ref[pl.ds(pl.multiple_of(at_e + i * blk, 8), blk), :n_j] = dot(fb, dg_ref[...].reshape(n * n_t, n_j), 0, 0)
        return c
    lax.fori_loop(0, 4, enc_block, 0)
    put(e_ref.at[pl.ds(at_e, n_e), pl.ds(0, n_j)], gwe_out)
    arp.ag1_mid()
    ar0.finish()
    for q in range(n_h // LANES):
        e_ref[at_o:at_o + n_j, q * LANES:(q + 1) * LANES] = s_out[q * n_j:(q + 1) * n_j]
    put(e_ref.at[pl.ds(at_o, n_j), pl.ds(0, n_h)], gwo_out.at[:, pl.ds(0, n_h)])
    ar1.finish()
    for q in range(n_h // LANES, n_v // LANES):
        e_ref[at_o:at_o + n_j, q * LANES:(q + 1) * LANES] = s_out[q * n_j:(q + 1) * n_j]
    put(e_ref.at[pl.ds(at_o, n_j), pl.ds(n_h, n_h)], gwo_out.at[:, pl.ds(n_h, n_h)])
    arp.d2d_back()
    arp.finish()
    n_g = g_ref.shape[1]
    for q in range(n_j // LANES):
        e_ref[at_p:at_p + n_g, q * LANES:(q + 1) * LANES] = s_pred[q * n_g:(q + 1) * n_g]
    put(e_ref.at[pl.ds(at_p, n_g), pl.ds(0, n_j)], gwp_out)

    pltpu.make_async_copy(abuf.at[others], a_ref.at[others], asend).wait()
    pltpu.make_async_copy(dabuf.at[others], darecv.at[others], dsend).wait()
    comm.drain()
    for cp in flush:
        cp.wait()


def move(*refs):
    half = len(refs) // 2
    for src, dst in zip(refs[:half], refs[half:]):
        dst[...] = src[...]


def solution(mesh):
    n = mesh.shape['seq']
    assert n == 2 * SIDE * SIDE
    parts = 2 * n

    def local_fn(enc_out, pred_out, w_enc, w_pred, w_out, labels, frame_len, label_len):
        n_utt, n_loc, n_e = enc_out.shape
        _, n_u, n_g = pred_out.shape
        n_j, n_v = w_out.shape
        n_t = n_loc * n
        assert n_utt == n
        m_o, m_p = pieces_rows(n_j, n_v // 2, parts), pieces_rows(n_g, n_j, parts)
        vm = pl.BlockSpec(memory_space=pltpu.VMEM)
        sm = pl.BlockSpec(memory_space=pltpu.SMEM)
        hbm = pl.BlockSpec(memory_space=pl.ANY)

        def ar_scratch(m):
            return [pltpu.VMEM((2, SIDE, SIDE, m, LANES), F32), pltpu.VMEM((2, 6, 2, m, LANES), F32), pltpu.VMEM((2, 3, m, LANES), F32)]
        hf = pltpu.VMEM((n_u, LANES), F32)
        n_sem = 3 * 34 + 2 * 15
        row = pltpu.VMEM((n, n_loc, 1, n_j), F32)
        msg = pltpu.VMEM((n, n_loc + 1, 1, n_j), F32)
        levels = [pltpu.VMEM((2 ** lv + 1, LANES >> lv, LANES), F32) for lv in range(LEVELS + 1)]
        shapes = tuple(jax.ShapeDtypeStruct(*a) for a in (((1, n), F32), ((n_utt, n_loc, n_e), BF16), ((n_e, n_j), F32), ((n_g, n_j), F32), ((n_j, n_v), F32)))
        outs = pl.pallas_call(
            functools.partial(kernel, n),
            out_shape=shapes,
            in_specs=[hbm, hbm, hbm, hbm, hbm, vm, sm, sm],
            out_specs=(hbm,) * 5,
            scratch_shapes=[
                pltpu.VMEM((n_utt, n_loc, n_e), BF16), pltpu.VMEM((n_e, n_j), BF16), pltpu.VMEM((n_g, n_j), BF16), pltpu.VMEM((n_j, n_v), BF16),
                pltpu.VMEM((n_u, n_g), BF16), row, row, pltpu.VMEM((n_t, n_j), F32),
                pltpu.VMEM((n_u, n_j), F32), pltpu.VMEM((n_u, n_v), F32), pltpu.VMEM((n_t * n_u, n_j), BF16),
                pltpu.VMEM((BLK_T * n_u, n_v), F32), pltpu.VMEM((BLK_T * n_u, n_v), F32),
                pltpu.VMEM((n_t * n_u, n_v), F32), hf, hf, hf,
                *levels, pltpu.VMEM((LANES + 8, LANES), F32), pltpu.VMEM((LANES + 8, LANES), F32), hf, hf, hf,
                pltpu.VMEM((n_t * n_u, n_v // 2), BF16), pltpu.VMEM((n_t * n_u, n_v // 2), BF16), pltpu.VMEM((n_u, n_j), F32),
                msg, msg, pltpu.VMEM((n_t, n_j), F32), pltpu.VMEM((n, n), F32), pltpu.VMEM((1, n), F32), pltpu.VMEM((n_utt, n_loc, n_e), BF16),
                pltpu.VMEM((2, 2, SIDE, SIDE, n, n_e), BF16), pltpu.VMEM((2, 2, SIDE, SIDE, n, n_j), BF16),
                pltpu.VMEM((2 * parts * m_o, LANES), F32), pltpu.VMEM((parts * m_p, LANES), F32),
                pltpu.VMEM((2 * parts * m_o, LANES), F32), pltpu.VMEM((parts * m_p, LANES), F32),
                *ar_scratch(m_o), *ar_scratch(m_o), *ar_scratch(m_p),
                pltpu.SemaphoreType.DMA((5,)), pltpu.SemaphoreType.DMA((6,)),
                pltpu.SemaphoreType.DMA, pltpu.SemaphoreType.DMA, pltpu.SemaphoreType.DMA, pltpu.SemaphoreType.DMA,
                pltpu.SemaphoreType.DMA((32,)), pltpu.SemaphoreType.DMA((n_sem,))],
            compiler_params=pltpu.CompilerParams(collective_id=0, has_side_effects=True, vmem_limit_bytes=63 * 1024 * 1024),
        )(enc_out, pred_out, w_enc, w_pred, w_out, labels, frame_len, label_len)
        steps = 8
        specs = tuple(pl.BlockSpec((o.shape[0] // steps,) + o.shape[1:], lambda i, d=len(o.shape): (i,) + (0,) * (d - 1)) if o.shape[0] > 1 else
                      pl.BlockSpec(o.shape, lambda i: (0, 0)) for o in shapes)
        loss, genc, gwe, gwp, gwo = pl.pallas_call(move, grid=(steps,), out_shape=shapes, in_specs=list(specs), out_specs=specs)(*outs)
        return loss.reshape(n), genc, gwe, gwp, gwo

    in_specs = (P('dp', 'seq', None), P('dp', None, None), P(None, None), P(None, None), P(None, None), P('dp', None), P('dp'), P('dp'))
    out_specs = (P('dp'), P('dp', 'seq', None), P('dp', None), P('dp', None), P('dp', None))
    return jax.shard_map(local_fn, mesh=mesh, in_specs=in_specs, out_specs=out_specs, check_vma=False)
```

time: 144 us -> 102 us (0.71)
  Pallas kernels: 125 us -> 101 us
  local copies, waits for them, and re-layouts: 18.4 us -> 0 us
    pallas_call x1 -> x2, Pallas kernels: 125 us -> 101 us  [the longest x1 93.1 us: local_fn(): pl.pallas_call(functools.partial(kernel, n), out_shape=shapes, in_specs=[...]
    reshape x3 -> x0, local copies, waits for them, and re-layouts: 6.8 us -> none  [the longest x1 3.59 us: unflat(): full.reshape(-1, LANES)[:r * c // LANES].reshape(c // LANES, r, LANES)]
    unnamed x2 -> x0, local copies, waits for them, and re-layouts: 3.78 us -> none
    slice x2 -> x0, local copies, waits for them, and re-layouts: 2.88 us -> none  [the longest x1 1.54 us: unflat(): full.reshape(-1, LANES)[:r * c // LANES].reshape(c // LANES, r, LANES)]
    another operation x1 -> x0, local copies, waits for them, and re-layouts: 2.16 us -> none  [unflat(): full.reshape(-1, LANES)[:r * c // LANES].reshape(c // LANES, r, LANES)]
    transpose x1 -> x0, local copies, waits for them, and re-layouts: 1.44 us -> none  [unflat(): full.reshape(-1, LANES)[:r * c // LANES].reshape(c // LANES, r, LANES)]
where the time goes in v2:
time: 102 us
  Pallas kernels  101 us (99%)
    pallas_call x1, Pallas kernels, local_fn(): pl.pallas_call(functools.partial(kernel, n), out_shape=shapes, in_specs=[...  93.1 us
    pallas_call x1, Pallas kernels, local_fn(): pl.pallas_call(move, grid=(steps,), out_shape=shapes, in_specs=list(specs...  8.16 us

profile of v2, /device:TPU:97, one launch (start us, length us, event | category | flops | bytes accessed | tf_op | source)
XLA Modules:
  0.0 101.9 jit_solution(16527105791931770522)
XLA Ops:
  0.6 93.1 %shard_map.119 = (f32[1,32]{1,0:T(1,128)}, bf16[32,2,1024]{2,1,0:T(2,128)(2,1)}, f32[1024,640]{1,0:T(8,128)}, f32[640,640]{1,0:T(8,128)}, f32[640,1024]{1,0:T(8,128)}) custom-call(bf16[32,2,1024]{2,1,0:T(2,128)(2,1)} %f_hbm.1, bf16[32,64,640]{2,1,0:T(8,128)(2,1)} %pred_ref.1, bf16[1024,640]{1,0:T(8,128)(2,1)} %we_hbm.1, bf16[640,640]{1,0:T(8,128)(2,1)} %wp_hbm.1, ...), custom_call_target="tpu_custom_call" | custom-call | tf_op jit(solution)/shard_map/pallas_call | solution.py:610
  93.7 8.2 %shard_map.120 = (f32[1,32]{1,0:T(1,128)}, bf16[32,2,1024]{2,1,0:T(2,128)(2,1)}, f32[1024,640]{1,0:T(8,128)}, f32[640,640]{1,0:T(8,128)}, f32[640,1024]{1,0:T(8,128)}) custom-call(f32[1,32]{1,0:T(1,128)} %get-tuple-element.15.refs_0_, bf16[32,2,1024]{2,1,0:T(2,128)(2,1)} %get-tuple-element.16.refs_1_, f32[1024,640]{1,0:T(8,128)} %get-tuple-element.17.refs_2_, ...), custom_call_target="tpu_custom_call" | custom-call | tf_op jit(solution)/shard_map/pallas_call | solution.py:636

commit v3 on v2

--- a/solution.py
+++ b/solution.py
@@ -105,13 +105,15 @@
 
 
 class AllReduce:
-    def __init__(self, comm, pos, full, part=None, r0=None, r1=None, r2=None):
+    def __init__(self, comm, pos, full, part=None, r0=None, r1=None, r2=None, relay=False):
         self.comm, (self.core, x, y, dev) = comm, pos
-        self.part, self.full, self.r0, self.r1, self.r2 = part, full, r0, r1, r2
+        self.part, self.full, self.r0, self.r1, self.r2, self.relay = part, full, r0, r1, r2, relay
         rx = Ring(x, lambda i: dev(i, y, self.core))
         ry = Ring(y, lambda i: dev(x, i, self.core))
         self.rings = ((rx, ry), (ry, rx))
         self.sibling = dev(x, y, 1 - self.core)
+        n = full.shape[4]
+        self.spans = ((0, n // 32 * 16), (n // 32 * 16, n - n // 32 * 16))
 
     def v1(self, ref, k):
         return lambda a, half: ref.at[self.core, k, a, pl.ds(2 * half, 2)]
@@ -119,18 +121,28 @@
     def v2(self, ref, k):
         return lambda b: ref.at[self.core, k, self.rings[k][0].me, b]
 
+    def v2h(self, ref, k):
+        return lambda b, half: ref.at[self.core, k, self.rings[k][0].me, b, pl.ds(*self.spans[half])]
+
     def b1(self, k):
         return [self.r1.at[k, s] for s in range(6)]
 
     def b2(self, k):
         return [self.r2.at[k, s] for s in range(3)]
 
+    def b2h(self, k):
+        return [self.r2.at[k, s, pl.ds(*self.spans[half])] for s, half in enumerate((0, 1, 1, 0, 0, 1))]
+
+    def mine(self, k):
+        return self.full.at[self.core, k, self.rings[k][0].me, self.rings[k][1].me]
+
     def d2d_start(self):
         self.st0 = self.comm.send(self.part.at[1 - self.core], self.r0, self.sibling)
 
     def rs1_start(self):
-        self.st0.wait_recv()
-        self.part[pl.ds(self.core, 1)] += self.r0[...][None]
+        if self.r0 is not None:
+            self.st0.wait_recv()
+            self.part[pl.ds(self.core, 1)] += self.r0[...][None]
         self.st = [rs_start(self.comm, self.rings[k][0], self.v1(self.part, k), self.b1(k)) for k in range(2)]
 
     def rs1_mid(self):
@@ -143,24 +155,40 @@
             def put(half, val, view=view, k=k):
                 view(self.rings[k][0].me, half)[...] = val
             rs_end(self.rings[k][0], view, self.b1(k), self.st[k], put)
-            self.st[k] = ex_start(self.comm, self.rings[k][1], self.v2(self.part, k), self.b2(k))
-
-    def mine(self, k):
-        return self.full.at[self.core, k, self.rings[k][0].me, self.rings[k][1].me]
+            if self.relay:
+                self.st[k] = rs_start(self.comm, self.rings[k][1], self.v2h(self.part, k), self.b2h(k))
+            else:
+                self.st[k] = ex_start(self.comm, self.rings[k][1], self.v2(self.part, k), self.b2(k))
+
+    def rs2_mid(self):
+        self.st = [rs_mid(self.comm, self.rings[k][1], self.v2h(self.part, k), self.b2h(k), self.st[k]) for k in range(2)]
+
+    def ag2_start(self):
+        for k in range(2):
+            if self.relay:
+                dst = self.v2h(self.full, k)
+
+                def put(half, val, dst=dst, k=k):
+                    dst(self.rings[k][1].me, half)[...] = val
+                rs_end(self.rings[k][1], self.v2h(self.part, k), self.b2h(k), self.st[k], put)
+            else:
+                for cp in self.st[k]:
+                    cp.wait_recv()
+                got = self.b2(k)
+                self.mine(k)[...] = self.v2(self.part, k)(self.rings[k][1].me)[...] + got[0][...] + got[1][...] + got[2][...]
+        self.gather_start()
 
     def gather_start(self):
         self.st = []
         for k in range(2):
-            own = self.mine(k)
-            self.st.append(ex_start(self.comm, self.rings[k][1], lambda b, own=own: own, (own, own, own)))
-
-    def ag2_start(self):
-        for k in range(2):
-            for cp in self.st[k]:
-                cp.wait_recv()
-            got = self.b2(k)
-            self.mine(k)[...] = self.v2(self.part, k)(self.rings[k][1].me)[...] + got[0][...] + got[1][...] + got[2][...]
-        self.gather_start()
+            own, ring = self.mine(k), self.rings[k][1]
+            if self.relay:
+                self.st.append((self.comm.send(own, own, ring.right), self.comm.send(own, own, ring.left)))
+            else:
+                self.st.append(ex_start(self.comm, ring, lambda b, own=own: own, (own, own, own)))
+
+    def ag2_mid(self):
+        self.st = [ag_mid(self.comm, self.rings[k][1], self.v2h(self.full, k), self.st[k]) for k in range(2)]
 
     def ag1_start(self):
         for k in range(2):
@@ -244,14 +272,15 @@
 
 
 LEVELS = 3
+BLK_G = 2
 
 
 def kernel(n, f_hbm, pred_ref, we_hbm, wp_hbm, wo_hbm, lab_ref, flen_ref, llen_ref,
            loss_out, genc_out, gwe_out, gwp_out, gwo_out,
            f_ref, we_ref, wp_ref, wo_ref, g_ref, abuf, a_ref, act_ref, c_ref, onehot_ref, h_ref, z0_ref, z1_ref, e_ref, bt_ref, lt_ref, rs_ref,
-           w0, w1, w2, w3, al_ref, be_ref, c1_ref, gb_ref, gl_ref, dz0_ref, dz1_ref, dc_ref, dabuf, darecv, daloc, loss_col, lossbuf, genc_ref,
-           fg_ref, dg_ref, p_out, p_pred, s_out, s_pred, r0a, r1a, r2a, r0b, r1b, r2b, r0p, r1p, r2p,
-           insem, outsem, asend, arecv, dsend, drecv, ssem, rsem):
+           w0, w1, w2, w3, al_ref, be_ref, c1_ref, gb_ref, gl_ref, dz_ref, dc_ref, dabuf, darecv,
+           fg_ref, dg_ref, p_out, p_pred, r0a, r1a, r2a, r1p, r2p,
+           insem, asend, arecv, dsend, drecv, ssem, rsem):
     me = lax.axis_index('seq')
     core, x, y = me % 2, (me // 2) % SIDE, me // (2 * SIDE)
 
@@ -263,27 +292,26 @@
     tl = n_t // n
     rows = BLK_T * n_u
     n_blk = n_t // BLK_T
-    n_h = n_v // 2
 
     barrier = pltpu.get_barrier_semaphore()
 
+    loads = [pltpu.make_async_copy(src, dst, insem.at[k]) for k, (src, dst) in enumerate(
+        ((f_hbm, f_ref), (we_hbm, we_ref), (pred_ref.at[pl.ds(me - core, 2)], g_ref), (wp_hbm, wp_ref), (wo_hbm, wo_ref)))]
+    for cp in loads:
+        cp.start()
     def greet(p, c):
         pl.semaphore_signal(barrier, inc=1, device_id={'seq': (me + p) % n}, device_id_type=pl.DeviceIdType.MESH)
         return c
     lax.fori_loop(1, n, greet, 0)
-    loads = [pltpu.make_async_copy(src, dst, insem.at[k]) for k, (src, dst) in enumerate(
-        ((f_hbm, f_ref), (we_hbm, we_ref), (pred_ref.at[me], g_ref), (wp_hbm, wp_ref), (wo_hbm, wo_ref)))]
-    for cp in loads:
-        cp.start()
     comm = Comm(ssem, rsem)
     pos = (core, x, y, dev)
 
     def six(ref, base, m):
         return ref.at[pl.ds(base, 64 * m)].reshape(2, 2, SIDE, SIDE, m, LANES)
-    m_o, m_p = n_j * n_h // LANES // 64, p_pred.shape[0] // 64
-    ar0 = AllReduce(comm, pos, six(s_out, 0, m_o), six(p_out, 0, m_o), r0a, r1a, r2a)
-    ar1 = AllReduce(comm, pos, six(s_out, 64 * m_o, m_o), six(p_out, 64 * m_o, m_o), r0b, r1b, r2b)
-    arp = AllReduce(comm, pos, six(s_pred, 0, m_p), six(p_pred, 0, m_p), r0p, r1p, r2p)
+    m_o, m_p = n_j * n_v // LANES // 64, p_pred.shape[0] // 64
+    at_p = 64 * m_o
+    aro = AllReduce(comm, pos, six(e_ref, 0, m_o), six(p_out, 0, m_o), r0a, r1a, r2a, relay=True)
+    arp = AllReduce(comm, pos, six(e_ref, at_p, m_p), six(p_pred, 0, m_p), None, r1p, r2p)
     agf = AllReduce(comm, pos, fg_ref)
     agd = AllReduce(comm, pos, dg_ref)
 
@@ -315,7 +343,7 @@
 
     loads[2].wait()
     loads[3].wait()
-    c_ref[...] = dot(g_ref[...], wp_ref[...], 1, 0).astype(BF16).astype(F32)
+    c_ref[...] = dot(g_ref[core], wp_ref[...], 1, 0).astype(BF16).astype(F32)
     n_lab = lab_ref.shape[1]
     u_row = lax.broadcasted_iota(jnp.int32, (n_u, n_lab), 0)
     u_col = lax.broadcasted_iota(jnp.int32, (n_u, n_lab), 1)
@@ -347,7 +375,8 @@
             e = jnp.exp(zt - m)
             s = jnp.sum(e, axis=1, keepdims=True)
             zl = jnp.sum(zt * onehot_ref[...], axis=1, keepdims=True)
-            e_ref[pl.ds(t * n_u, n_u), :] = e
+            for q in range(n_v // LANES):
+                e_ref[pl.ds(q * n_t * n_u + t * n_u, n_u), :] = e[:, q * LANES:(q + 1) * LANES]
             norm = m + jnp.log(s)
             here = lane == t
             bt_ref[...] = jnp.where(here, zt[:, :1] - norm, bt_ref[...])
@@ -368,7 +397,6 @@
     scores(n_blk - 1, z1_ref)
     stats(n_blk - 2, z0_ref)
     stats(n_blk - 1, z1_ref)
-    agf.ag1_mid()
 
     t_len = flen_ref[me]
     u_len = llen_ref[me]
@@ -400,57 +428,45 @@
     gl_ref[...] = gl
     c1_ref[...] = (gb + gl) * rs_ref[...]
 
-    for b in range(n):
-        dabuf[b, tl] = jnp.broadcast_to(-logp, (1, n_j))
-    dc_ref[...] = jnp.zeros_like(dc_ref)
-    p_out[...] = jnp.zeros_like(p_out)
+    dc_ref[core] = jnp.zeros(dc_ref.shape[1:], F32)
+    dc_ref[core, n_u:n_u + 1, :] = jnp.broadcast_to(-logp, (1, n_j))
     v0 = lax.broadcasted_iota(jnp.int32, (n_u, LANES), 1) == 0
 
-    def grad_logits(i, lo, dz_ref):
+    def grad_logits(i):
         turn = (LANES - i * BLK_T) % LANES
         c1 = pltpu.roll(c1_ref[...], turn, 1)
         gbr = pltpu.roll(gb_ref[...], turn, 1)
         glr = pltpu.roll(gl_ref[...], turn, 1)
         for k in range(BLK_T):
             at = (i * BLK_T + k) * n_u
-            dz = e_ref[pl.ds(at, n_u), lo:lo + n_h] * c1[:, k:k + 1] - glr[:, k:k + 1] * onehot_ref[:, lo:lo + n_h]
-            if lo == 0:
-                dz_ref[pl.ds(at, n_u), LANES:] = dz[:, LANES:].astype(BF16)
-                dz_ref[pl.ds(at, n_u), :LANES] = (dz[:, :LANES] - jnp.where(v0, gbr[:, k:k + 1], 0.0)).astype(BF16)
-            else:
-                dz_ref[pl.ds(at, n_u), :] = dz.astype(BF16)
-
-    def grad_out(i, q0, dz_ref):
-        hb = h_ref[pl.ds(i * 2 * rows, 2 * rows), :]
-        r = dot(hb, dz_ref[pl.ds(i * 2 * rows, 2 * rows), :], 0, 0)
-        for q in range(n_h // LANES):
-            p_out[(q0 + q) * n_j:(q0 + q + 1) * n_j] += r[:, q * LANES:(q + 1) * LANES]
-
-    def phase0(i, c):
-        grad_logits(i, 0, dz0_ref)
-        return c
-
-    def phase1(i, c):
-        grad_out(i, 0, dz0_ref)
-        grad_logits(2 * i, n_h, dz1_ref)
-        grad_logits(2 * i + 1, n_h, dz1_ref)
-        return c
-
-    def phase2(i, c):
-        grad_out(i, n_h // LANES, dz1_ref)
-        return c
+            for q in range(n_v // LANES):
+                cols = slice(q * LANES, (q + 1) * LANES)
+                dz = e_ref[q * n_t * n_u + at:q * n_t * n_u + at + n_u, :] * c1[:, k:k + 1] - glr[:, k:k + 1] * onehot_ref[:, cols]
+                if q == 0:
+                    dz = dz - jnp.where(v0, gbr[:, k:k + 1], 0.0)
+                dz_ref[at:at + n_u, cols] = dz.astype(BF16)
+
+    def grad_out(i):
+        at = slice(i * BLK_G * rows, (i + 1) * BLK_G * rows)
+        r = dot(h_ref[at, :], dz_ref[at, :], 0, 0)
+        for q in range(n_v // LANES):
+            part = r[:, q * LANES:(q + 1) * LANES]
+            p_out[q * n_j:(q + 1) * n_j] = part if i == 0 else p_out[q * n_j:(q + 1) * n_j] + part
 
     def grad_hidden(i, z_ref):
-        at = pl.ds(i * rows, rows)
-        z_ref[:, :n_j] = dot(dz0_ref[at, :], wo_ref[:, :n_h], 1, 1) + dot(dz1_ref[at, :], wo_ref[:, n_h:], 1, 1)
+        z_ref[:, :n_j] = dot(dz_ref[pl.ds(i * rows, rows), :], wo_ref[...], 1, 1)
 
     def grad_pre(i, z_ref):
+        row = []
         for k in range(BLK_T):
             t = i * BLK_T + k
             hf = h_ref[pl.ds(t * n_u, n_u), :].astype(F32)
             dpt = (z_ref[k * n_u:(k + 1) * n_u, :n_j] * (1.0 - hf * hf)).astype(BF16).astype(F32)
-            dabuf[t // tl, t % tl] = jnp.sum(dpt, axis=0, keepdims=True).astype(BF16).astype(F32)
-            dc_ref[...] += dpt
+            row.append(jnp.sum(dpt, axis=0, keepdims=True))
+            if len(row) == tl:
+                dabuf[t // tl] = jnp.concatenate(row, axis=0).astype(BF16)
+                row = []
+            dc_ref[core, :n_u, :] += dpt
 
     def phase3(i, c):
         grad_hidden(2 * i + 1, z1_ref)
@@ -459,30 +475,28 @@
         grad_pre(2 * i + 1, z1_ref)
         return c
 
-    lax.fori_loop(0, n_blk, phase0, 0)
-    agf.d2d_back()
-    lax.fori_loop(0, n_blk // 2, phase1, 0)
-    ar0.d2d_start()
-    lax.fori_loop(0, n_blk // 4, phase2, 0)
-    ar0.rs1_start()
-    lax.fori_loop(n_blk // 4, n_blk // 2, phase2, 0)
-    ar1.d2d_start()
+    for k in range(BLK_G):
+        grad_logits(k)
+    agf.ag1_mid()
+    for i in range(n_blk // BLK_G):
+        grad_out(i)
+        if i + 1 < n_blk // BLK_G:
+            for k in range(BLK_G):
+                grad_logits(BLK_G * (i + 1) + k)
+    aro.d2d_start()
     grad_hidden(0, z0_ref)
     lax.fori_loop(0, 1, phase3, 0)
-    ar1.rs1_start()
-    ar0.rs1_mid()
-    lax.fori_loop(1, 2, phase3, 0)
-    ar1.rs1_mid()
-    lax.fori_loop(2, n_pair, phase3, 0)
-    ar0.rs2_start()
+    aro.rs1_start()
+    agf.d2d_back()
+    lax.fori_loop(1, n_pair, phase3, 0)
     grad_hidden(n_blk - 1, z1_ref)
     grad_pre(n_blk - 2, z0_ref)
     grad_pre(n_blk - 1, z1_ref)
 
-    def keep(k, c):
-        darecv[me, k] = dabuf[me, k]
-        return c
-    lax.fori_loop(0, tl + 1, keep, 0)
+    own_dc = dc_ref.at[core]
+    dc_copy = comm.send(own_dc, own_dc, aro.sibling)
+    darecv[me] = dabuf[me]
+    aro.rs1_mid()
 
     def d_copy(p):
         to = (me + p) % n
@@ -493,94 +507,82 @@
         return c
     lax.fori_loop(1, n, d_go, 0)
 
-    gwp = dot(g_ref[...], dc_ref[...].astype(BF16), 0, 0)
+    dc_copy.wait_recv()
+    n_g = g_ref.shape[2]
+    gwp = dot(g_ref[...].reshape(2 * n_u, n_g), dc_ref[:, :n_u, :].reshape(2 * n_u, n_j).astype(BF16), 0, 0)
     for q in range(n_j // LANES):
-        p_pred[q * n_j:(q + 1) * n_j] = gwp[:, q * LANES:(q + 1) * LANES]
-    used = n_j * n_j // LANES
-    if used < p_pred.shape[0]:
-        p_pred[used:] = jnp.zeros((p_pred.shape[0] - used, LANES), F32)
-    arp.d2d_start()
-    ar1.rs2_start()
-    ar0.ag2_start()
+        p_pred[q * n_g:(q + 1) * n_g] = gwp[:, q * LANES:(q + 1) * LANES]
+    used = n_g * n_j // LANES
+    spare = lax.broadcasted_iota(jnp.int32, (p_pred.shape[0] - used, LANES), 0) - me + core
+    p_pred[used:] = jnp.where(spare == 0, dc_ref[0, n_u:n_u + 1, :LANES], jnp.where(spare == 1, dc_ref[1, n_u:n_u + 1, :LANES], 0.0))
     arp.rs1_start()
-    ar1.ag2_start()
+    aro.rs2_start()
     pltpu.make_async_copy(dabuf.at[others], darecv.at[others], drecv).wait()
 
-    def collect(b, c):
-        for k in range(tl):
-            daloc[pl.ds(k * n + b, 1), :] = darecv[b, k]
-        loss_col[pl.ds(b, 1), :] = darecv[b, tl][:, :n]
-        return c
-    lax.fori_loop(0, n, collect, 0)
-    dal = daloc[...].astype(BF16)
+    dal = jnp.concatenate([darecv[:, k, :] for k in range(tl)], axis=0)
     for k in range(2):
         agd.mine(k)[...] = dal[k * n:(k + 1) * n, :]
     agd.gather_start()
-    ar0.ag1_start()
-    arp.rs1_mid()
-    diag = lax.broadcasted_iota(jnp.int32, (n, n), 0) == lax.broadcasted_iota(jnp.int32, (n, n), 1)
-    lossbuf[...] = jnp.sum(jnp.where(diag, loss_col[...], 0.0), axis=0, keepdims=True)
+    aro.rs2_mid()
     genc = dot(dal, we_ref[...], 1, 1).astype(BF16)
     for k in range(tl):
-        genc_ref[:, k, :] = genc[k * n:(k + 1) * n, :]
-    flush = []
-
-    def put(src, dst):
-        cp = pltpu.make_async_copy(src, dst, outsem.at[len(flush)])
-        cp.start()
-        flush.append(cp)
-    put(lossbuf, loss_out)
-    put(genc_ref, genc_out)
+        genc_out[:, k, :] = genc[k * n:(k + 1) * n, :]
+    arp.rs1_mid()
     agd.ag1_start()
-    ar0.ag1_mid()
-    ar1.ag1_start()
+    aro.ag2_start()
     arp.rs2_start()
+    aro.ag2_mid()
     agd.ag1_mid()
-    ar1.ag1_mid()
     arp.ag2_start()
-    ar0.d2d_back()
+    aro.ag1_start()
     agd.d2d_back()
-    ar1.d2d_back()
+
+    blk = n_e // 4
+
+    def enc_block(i, side, first):
+        fb = fg_ref[side, :, :, :, :, pl.ds(pl.multiple_of(i * blk, blk), blk)].reshape(n * n_t // 2, blk)
+        r = dot(fb, dg_ref[side].reshape(n * n_t // 2, n_j), 0, 0)
+        at = pl.ds(pl.multiple_of(i * blk, blk), blk)
+        gwe_out[at, :] = r if first else gwe_out[at, :] + r
+
+    def enc_own(i, c):
+        enc_block(i, core, True)
+        return c
+
+    def enc_other(i, c):
+        enc_block(i, 1 - core, False)
+        return c
+
+    def put_cols(base, n_r, dst):
+        for q in range(dst.shape[1] // LANES):
+            dst[:, q * LANES:(q + 1) * LANES] = e_ref[base + q * n_r:base + (q + 1) * n_r]
+    lax.fori_loop(0, 4, enc_own, 0)
     arp.ag1_start()
+    aro.ag1_mid()
     agf.finish()
     agd.finish()
-
-    at_o, at_e, at_p = 0, n_j, n_j + n_e
-    blk = n_e // 4
-
-    def enc_block(i, c):
-        fb = fg_ref[:, :, :, :, :, pl.ds(pl.multiple_of(i * blk, blk), blk)].reshape(n * n_t, blk)
-        e_ref[pl.ds(pl.multiple_of(at_e + i * blk, 8), blk), :n_j] = dot(fb, dg_ref[...].reshape(n * n_t, n_j), 0, 0)
-        return c
-    lax.fori_loop(0, 4, enc_block, 0)
-    put(e_ref.at[pl.ds(at_e, n_e), pl.ds(0, n_j)], gwe_out)
+    lax.fori_loop(0, 4, enc_other, 0)
     arp.ag1_mid()
-    ar0.finish()
-    for q in range(n_h // LANES):
-        e_ref[at_o:at_o + n_j, q * LANES:(q + 1) * LANES] = s_out[q * n_j:(q + 1) * n_j]
-    put(e_ref.at[pl.ds(at_o, n_j), pl.ds(0, n_h)], gwo_out.at[:, pl.ds(0, n_h)])
-    ar1.finish()
-    for q in range(n_h // LANES, n_v // LANES):
-        e_ref[at_o:at_o + n_j, q * LANES:(q + 1) * LANES] = s_out[q * n_j:(q + 1) * n_j]
-    put(e_ref.at[pl.ds(at_o, n_j), pl.ds(n_h, n_h)], gwo_out.at[:, pl.ds(n_h, n_h)])
+    aro.d2d_back()
     arp.d2d_back()
+    aro.finish()
+    put_cols(0, n_j, gwo_out)
     arp.finish()
-    n_g = g_ref.shape[1]
-    for q in range(n_j // LANES):
-        e_ref[at_p:at_p + n_g, q * LANES:(q + 1) * LANES] = s_pred[q * n_g:(q + 1) * n_g]
-    put(e_ref.at[pl.ds(at_p, n_g), pl.ds(0, n_j)], gwp_out)
-
+    put_cols(at_p, n_g, gwp_out)
+    diag = lax.broadcasted_iota(jnp.int32, (n, n), 0) == lax.broadcasted_iota(jnp.int32, (n, n), 1)
+    loss_out[...] = jnp.sum(jnp.where(diag, e_ref[at_p + used:at_p + used + n, :n], 0.0), axis=0, keepdims=True)
     pltpu.make_async_copy(abuf.at[others], a_ref.at[others], asend).wait()
     pltpu.make_async_copy(dabuf.at[others], darecv.at[others], dsend).wait()
     comm.drain()
-    for cp in flush:
+
+
+def move(count, *refs):
+    src, dst, sem = refs[:count], refs[count:2 * count], refs[2 * count]
+    copies = [pltpu.make_async_copy(a, b, sem.at[k]) for k, (a, b) in enumerate(zip(src, dst))]
+    for cp in copies:
+        cp.start()
+    for cp in copies:
         cp.wait()
-
-
-def move(*refs):
-    half = len(refs) // 2
-    for src, dst in zip(refs[:half], refs[half:]):
-        dst[...] = src[...]
 
 
 def solution(mesh):
@@ -594,46 +596,45 @@
         n_j, n_v = w_out.shape
         n_t = n_loc * n
         assert n_utt == n
-        m_o, m_p = pieces_rows(n_j, n_v // 2, parts), pieces_rows(n_g, n_j, parts)
+        m_o, m_p = pieces_rows(n_j, n_v, parts), pieces_rows(n_g, n_j, parts)
+        assert parts * m_p >= n_g * n_j // LANES + n
         vm = pl.BlockSpec(memory_space=pltpu.VMEM)
         sm = pl.BlockSpec(memory_space=pltpu.SMEM)
         hbm = pl.BlockSpec(memory_space=pl.ANY)
 
         def ar_scratch(m):
-            return [pltpu.VMEM((2, SIDE, SIDE, m, LANES), F32), pltpu.VMEM((2, 6, 2, m, LANES), F32), pltpu.VMEM((2, 3, m, LANES), F32)]
+            return [pltpu.VMEM((2, 6, 2, m, LANES), F32), pltpu.VMEM((2, 6, m, LANES), F32)]
         hf = pltpu.VMEM((n_u, LANES), F32)
-        n_sem = 3 * 34 + 2 * 15
+        n_sem = 42 + 33 + 2 * 15 + 1
         row = pltpu.VMEM((n, n_loc, 1, n_j), F32)
-        msg = pltpu.VMEM((n, n_loc + 1, 1, n_j), F32)
+        msg = pltpu.VMEM((n, n_loc, n_j), BF16)
         levels = [pltpu.VMEM((2 ** lv + 1, LANES >> lv, LANES), F32) for lv in range(LEVELS + 1)]
         shapes = tuple(jax.ShapeDtypeStruct(*a) for a in (((1, n), F32), ((n_utt, n_loc, n_e), BF16), ((n_e, n_j), F32), ((n_g, n_j), F32), ((n_j, n_v), F32)))
         outs = pl.pallas_call(
             functools.partial(kernel, n),
-            out_shape=shapes,
+            out_shape=tuple(pltpu.VMEM(o.shape, o.dtype) for o in shapes),
             in_specs=[hbm, hbm, hbm, hbm, hbm, vm, sm, sm],
-            out_specs=(hbm,) * 5,
+            out_specs=(vm,) * 5,
             scratch_shapes=[
                 pltpu.VMEM((n_utt, n_loc, n_e), BF16), pltpu.VMEM((n_e, n_j), BF16), pltpu.VMEM((n_g, n_j), BF16), pltpu.VMEM((n_j, n_v), BF16),
-                pltpu.VMEM((n_u, n_g), BF16), row, row, pltpu.VMEM((n_t, n_j), F32),
+                pltpu.VMEM((2, n_u, n_g), BF16), row, row, pltpu.VMEM((n_t, n_j), F32),
                 pltpu.VMEM((n_u, n_j), F32), pltpu.VMEM((n_u, n_v), F32), pltpu.VMEM((n_t * n_u, n_j), BF16),
                 pltpu.VMEM((BLK_T * n_u, n_v), F32), pltpu.VMEM((BLK_T * n_u, n_v), F32),
-                pltpu.VMEM((n_t * n_u, n_v), F32), hf, hf, hf,
+                pltpu.VMEM((n_t * n_u * n_v // LANES, LANES), F32), hf, hf, hf,
                 *levels, pltpu.VMEM((LANES + 8, LANES), F32), pltpu.VMEM((LANES + 8, LANES), F32), hf, hf, hf,
-                pltpu.VMEM((n_t * n_u, n_v // 2), BF16), pltpu.VMEM((n_t * n_u, n_v // 2), BF16), pltpu.VMEM((n_u, n_j), F32),
-                msg, msg, pltpu.VMEM((n_t, n_j), F32), pltpu.VMEM((n, n), F32), pltpu.VMEM((1, n), F32), pltpu.VMEM((n_utt, n_loc, n_e), BF16),
+                pltpu.VMEM((n_t * n_u, n_v), BF16), pltpu.VMEM((2, n_u + 8, n_j), F32),
+                msg, msg,
                 pltpu.VMEM((2, 2, SIDE, SIDE, n, n_e), BF16), pltpu.VMEM((2, 2, SIDE, SIDE, n, n_j), BF16),
-                pltpu.VMEM((2 * parts * m_o, LANES), F32), pltpu.VMEM((parts * m_p, LANES), F32),
-                pltpu.VMEM((2 * parts * m_o, LANES), F32), pltpu.VMEM((parts * m_p, LANES), F32),
-                *ar_scratch(m_o), *ar_scratch(m_o), *ar_scratch(m_p),
-                pltpu.SemaphoreType.DMA((5,)), pltpu.SemaphoreType.DMA((6,)),
+                pltpu.VMEM((parts * m_o, LANES), F32), pltpu.VMEM((parts * m_p, LANES), F32),
+                pltpu.VMEM((2, SIDE, SIDE, m_o, LANES), F32), *ar_scratch(m_o), *ar_scratch(m_p),
+                pltpu.SemaphoreType.DMA((5,)),
                 pltpu.SemaphoreType.DMA, pltpu.SemaphoreType.DMA, pltpu.SemaphoreType.DMA, pltpu.SemaphoreType.DMA,
-                pltpu.SemaphoreType.DMA((32,)), pltpu.SemaphoreType.DMA((n_sem,))],
-            compiler_params=pltpu.CompilerParams(collective_id=0, has_side_effects=True, vmem_limit_bytes=63 * 1024 * 1024),
+                pltpu.SemaphoreType.DMA((48,)), pltpu.SemaphoreType.DMA((n_sem,))],
+            compiler_params=pltpu.CompilerParams(collective_id=0, has_side_effects=True, vmem_limit_bytes=57 * 1024 * 1024 - 128 * 1024),
         )(enc_out, pred_out, w_enc, w_pred, w_out, labels, frame_len, label_len)
-        steps = 8
-        specs = tuple(pl.BlockSpec((o.shape[0] // steps,) + o.shape[1:], lambda i, d=len(o.shape): (i,) + (0,) * (d - 1)) if o.shape[0] > 1 else
-                      pl.BlockSpec(o.shape, lambda i: (0, 0)) for o in shapes)
-        loss, genc, gwe, gwp, gwo = pl.pallas_call(move, grid=(steps,), out_shape=shapes, in_specs=list(specs), out_specs=specs)(*outs)
+        loss, genc, gwe, gwp, gwo = pl.pallas_call(
+            functools.partial(move, len(shapes)), out_shape=shapes, in_specs=[vm] * len(shapes), out_specs=(hbm,) * len(shapes),
+            scratch_shapes=[pltpu.SemaphoreType.DMA((len(shapes),))], compiler_params=pltpu.CompilerParams(vmem_limit_bytes=256 * 1024))(*outs)
         return loss.reshape(n), genc, gwe, gwp, gwo
 
     in_specs = (P('dp', 'seq', None), P('dp', None, None), P(None, None), P(None, None), P(None, None), P('dp', None), P('dp'), P('dp'))

time: 102 us -> 88.4 us (0.87)
  Pallas kernels: 101 us -> 87.4 us
    pallas_call x2, Pallas kernels: 101 us -> 87.4 us  [the longest x1 84.4 us: local_fn(): pl.pallas_call(functools.partial(kernel, n), out_shape=tuple((pltpu.VMEM(...]
where the time goes in v3:
time: 88.4 us; the launch traced here: 88.2 us
  Pallas kernels  87.4 us (99%)
    pallas_call x1, Pallas kernels, local_fn(): pl.pallas_call(functools.partial(kernel, n), out_shape=tuple((pltpu.VMEM(...  84.4 us
    pallas_call x1, Pallas kernels, local_fn(): pl.pallas_call(functools.partial(move, len(shapes)), out_shape=shapes, in...  2.99 us

profile of v3, /device:TPU:97, one launch (start us, length us, event | category | flops | bytes accessed | tf_op | source)
XLA Modules:
  0.0 88.2 jit_solution(13393596892700651088)
XLA Ops:
  0.6 84.4 %shard_map.119 = (f32[1,32]{1,0:T(1,128)S(1)}, bf16[32,2,1024]{2,1,0:T(2,128)(2,1)S(1)}, f32[1024,640]{1,0:T(8,128)S(1)}, f32[640,640]{1,0:T(8,128)S(1)}, f32[640,1024]{1,0:T(8,128)S(1)}) custom-call(bf16[32,2,1024]{2,1,0:T(2,128)(2,1)} %f_hbm.1, bf16[32,64,640]{2,1,0:T(8,128)(2,1)} %pred_ref.1, bf16[1024,640]{1,0:T(8,128)(2,1)} %we_hbm.1, ...), custom_call_target="tpu_custom_call" | custom-call | tf_op jit(solution)/shard_map/pallas_call | solution.py:613
  85.1 3.0 %shard_map.120 = (f32[1,32]{1,0:T(1,128)}, bf16[32,2,1024]{2,1,0:T(2,128)(2,1)}, f32[1024,640]{1,0:T(8,128)}, f32[640,640]{1,0:T(8,128)}, f32[640,1024]{1,0:T(8,128)}) custom-call(f32[1,32]{1,0:T(1,128)S(1)} %get-tuple-element.15.refs_0_, bf16[32,2,1024]{2,1,0:T(2,128)(2,1)S(1)} %get-tuple-element.16.refs_1_, f32[1024,640]{1,0:T(8,128)S(1)} %get-tuple-element.17.refs_2_, ...), custom_call_target="tpu_custom_call" | custom-call | tf_op jit(solution)/shard_map/pallas_call | solution.py:635

commit v4 on v3

--- a/solution.py
+++ b/solution.py
@@ -277,9 +277,9 @@
 
 def kernel(n, f_hbm, pred_ref, we_hbm, wp_hbm, wo_hbm, lab_ref, flen_ref, llen_ref,
            loss_out, genc_out, gwe_out, gwp_out, gwo_out,
-           f_ref, we_ref, wp_ref, wo_ref, g_ref, abuf, a_ref, act_ref, c_ref, onehot_ref, h_ref, z0_ref, z1_ref, e_ref, bt_ref, lt_ref, rs_ref,
+           f_ref, we_ref, wp_ref, wo_ref, g_ref, abuf, arecv_buf, a_ref, c_ref, onehot_ref, h_ref, z0_ref, z1_ref, e_ref, bt_ref, lt_ref, rs_ref,
            w0, w1, w2, w3, al_ref, be_ref, c1_ref, gb_ref, gl_ref, dz_ref, dc_ref, dabuf, darecv,
-           fg_ref, dg_ref, p_out, p_pred, r0a, r1a, r2a, r1p, r2p,
+           fg_ref, dg_ref, p_out, r0a, r1a, r2a, r1p, r2p,
            insem, asend, arecv, dsend, drecv, ssem, rsem):
     me = lax.axis_index('seq')
     core, x, y = me % 2, (me // 2) % SIDE, me // (2 * SIDE)
@@ -308,32 +308,29 @@
 
     def six(ref, base, m):
         return ref.at[pl.ds(base, 64 * m)].reshape(2, 2, SIDE, SIDE, m, LANES)
-    m_o, m_p = n_j * n_v // LANES // 64, p_pred.shape[0] // 64
+    m_o = n_j * n_v // LANES // 64
+    m_p = r2p.shape[2]
     at_p = 64 * m_o
+    p_pred = e_ref.at[pl.ds(at_p + 64 * m_p, 64 * m_p)]
     aro = AllReduce(comm, pos, six(e_ref, 0, m_o), six(p_out, 0, m_o), r0a, r1a, r2a, relay=True)
-    arp = AllReduce(comm, pos, six(e_ref, at_p, m_p), six(p_pred, 0, m_p), None, r1p, r2p)
+    arp = AllReduce(comm, pos, six(e_ref, at_p, m_p), six(e_ref, at_p + 64 * m_p, m_p), None, r1p, r2p)
     agf = AllReduce(comm, pos, fg_ref)
-    agd = AllReduce(comm, pos, dg_ref)
+    agd = AllReduce(comm, pos, dg_ref, relay=True)
 
     loads[0].wait()
     loads[1].wait()
     for k in range(tl):
         agf.mine(k)[...] = f_ref[:, k, :]
     f_loc = jnp.concatenate([agf.mine(k)[...] for k in range(tl)], axis=0)
-    act_ref[...] = dot(f_loc, we_ref[...], 1, 0).astype(BF16).astype(F32)
-
-    def spread(b, c):
-        for k in range(tl):
-            abuf[b, k] = act_ref[pl.ds(k * n + b, 1), :]
-        return c
-    lax.fori_loop(0, n, spread, 0)
+    act = dot(f_loc, we_ref[...], 1, 0).astype(BF16)
     for k in range(tl):
-        a_ref[me, k] = act_ref[pl.ds(k * n + me, 1), :]
+        abuf[:, k, :] = act[k * n:(k + 1) * n, :]
+    arecv_buf[me] = abuf[me]
     pl.semaphore_wait(barrier, n - 1)
 
     def a_copy(p):
         to = (me + p) % n
-        return pltpu.make_async_remote_copy(src_ref=abuf.at[to], dst_ref=a_ref.at[me], send_sem=asend, recv_sem=arecv, device_id={'seq': to}, device_id_type=pl.DeviceIdType.MESH)
+        return pltpu.make_async_remote_copy(src_ref=abuf.at[to], dst_ref=arecv_buf.at[me], send_sem=asend, recv_sem=arecv, device_id={'seq': to}, device_id_type=pl.DeviceIdType.MESH)
 
     def a_go(p, c):
         a_copy(p).start()
@@ -357,7 +354,14 @@
     loads[4].wait()
 
     others = pl.ds(0, n - 1)
-    pltpu.make_async_copy(abuf.at[others], a_ref.at[others], arecv).wait()
+    pltpu.make_async_copy(abuf.at[others], arecv_buf.at[others], arecv).wait()
+
+    def widen(b, c):
+        both = arecv_buf[b].astype(F32)
+        for k in range(tl):
+            a_ref[b, k] = both[k:k + 1, :]
+        return c
+    lax.fori_loop(0, n, widen, 0, unroll=4)
 
     lane = lax.broadcasted_iota(jnp.int32, (n_u, LANES), 1)
     u_sub = lax.broadcasted_iota(jnp.int32, (n_u, LANES), 0)
@@ -523,18 +527,20 @@
     for k in range(2):
         agd.mine(k)[...] = dal[k * n:(k + 1) * n, :]
     agd.gather_start()
+    arp.rs1_mid()
     aro.rs2_mid()
+    agd.ag2_mid()
     genc = dot(dal, we_ref[...], 1, 1).astype(BF16)
     for k in range(tl):
         genc_out[:, k, :] = genc[k * n:(k + 1) * n, :]
-    arp.rs1_mid()
+    arp.rs2_start()
+    aro.ag2_start()
     agd.ag1_start()
-    aro.ag2_start()
-    arp.rs2_start()
     aro.ag2_mid()
+    arp.ag2_start()
     agd.ag1_mid()
-    arp.ag2_start()
     aro.ag1_start()
+    arp.ag1_start()
     agd.d2d_back()
 
     blk = n_e // 4
@@ -557,12 +563,12 @@
         for q in range(dst.shape[1] // LANES):
             dst[:, q * LANES:(q + 1) * LANES] = e_ref[base + q * n_r:base + (q + 1) * n_r]
     lax.fori_loop(0, 4, enc_own, 0)
-    arp.ag1_start()
     aro.ag1_mid()
     agf.finish()
     agd.finish()
-    lax.fori_loop(0, 4, enc_other, 0)
+    lax.fori_loop(0, 2, enc_other, 0)
     arp.ag1_mid()
+    lax.fori_loop(2, 4, enc_other, 0)
     aro.d2d_back()
     arp.d2d_back()
     aro.finish()
@@ -571,7 +577,7 @@
     put_cols(at_p, n_g, gwp_out)
     diag = lax.broadcasted_iota(jnp.int32, (n, n), 0) == lax.broadcasted_iota(jnp.int32, (n, n), 1)
     loss_out[...] = jnp.sum(jnp.where(diag, e_ref[at_p + used:at_p + used + n, :n], 0.0), axis=0, keepdims=True)
-    pltpu.make_async_copy(abuf.at[others], a_ref.at[others], asend).wait()
+    pltpu.make_async_copy(abuf.at[others], arecv_buf.at[others], asend).wait()
     pltpu.make_async_copy(dabuf.at[others], darecv.at[others], dsend).wait()
     comm.drain()
 
@@ -605,7 +611,7 @@
         def ar_scratch(m):
             return [pltpu.VMEM((2, 6, 2, m, LANES), F32), pltpu.VMEM((2, 6, m, LANES), F32)]
         hf = pltpu.VMEM((n_u, LANES), F32)
-        n_sem = 42 + 33 + 2 * 15 + 1
+        n_sem = 42 + 33 + 17 + 15 + 1
         row = pltpu.VMEM((n, n_loc, 1, n_j), F32)
         msg = pltpu.VMEM((n, n_loc, n_j), BF16)
         levels = [pltpu.VMEM((2 ** lv + 1, LANES >> lv, LANES), F32) for lv in range(LEVELS + 1)]
@@ -617,7 +623,7 @@
             out_specs=(vm,) * 5,
             scratch_shapes=[
                 pltpu.VMEM((n_utt, n_loc, n_e), BF16), pltpu.VMEM((n_e, n_j), BF16), pltpu.VMEM((n_g, n_j), BF16), pltpu.VMEM((n_j, n_v), BF16),
-                pltpu.VMEM((2, n_u, n_g), BF16), row, row, pltpu.VMEM((n_t, n_j), F32),
+                pltpu.VMEM((2, n_u, n_g), BF16), msg, msg, row,
                 pltpu.VMEM((n_u, n_j), F32), pltpu.VMEM((n_u, n_v), F32), pltpu.VMEM((n_t * n_u, n_j), BF16),
                 pltpu.VMEM((BLK_T * n_u, n_v), F32), pltpu.VMEM((BLK_T * n_u, n_v), F32),
                 pltpu.VMEM((n_t * n_u * n_v // LANES, LANES), F32), hf, hf, hf,
@@ -625,7 +631,7 @@
                 pltpu.VMEM((n_t * n_u, n_v), BF16), pltpu.VMEM((2, n_u + 8, n_j), F32),
                 msg, msg,
                 pltpu.VMEM((2, 2, SIDE, SIDE, n, n_e), BF16), pltpu.VMEM((2, 2, SIDE, SIDE, n, n_j), BF16),
-                pltpu.VMEM((parts * m_o, LANES), F32), pltpu.VMEM((parts * m_p, LANES), F32),
+                pltpu.VMEM((parts * m_o, LANES), F32),
                 pltpu.VMEM((2, SIDE, SIDE, m_o, LANES), F32), *ar_scratch(m_o), *ar_scratch(m_p),
                 pltpu.SemaphoreType.DMA((5,)),
                 pltpu.SemaphoreType.DMA, pltpu.SemaphoreType.DMA, pltpu.SemaphoreType.DMA, pltpu.SemaphoreType.DMA,

time: 88.4 us -> 86.9 us (0.983)
  Pallas kernels: 87.4 us -> 85.9 us
    pallas_call x1, Pallas kernels: 84.4 us -> 82.9 us  [local_fn(): pl.pallas_call(functools.partial(kernel, n), out_shape=tuple((pltpu.VMEM(...]
where the time goes in v4:
time: 86.9 us; the launch traced here: 86.7 us
  Pallas kernels  85.9 us (99%)
    pallas_call x1, Pallas kernels, local_fn(): pl.pallas_call(functools.partial(kernel, n), out_shape=tuple((pltpu.VMEM(...  82.9 us
    pallas_call x1, Pallas kernels, local_fn(): pl.pallas_call(functools.partial(move, len(shapes)), out_shape=shapes, in...  2.99 us

profile of v4, /device:TPU:97, one launch (start us, length us, event | category | flops | bytes accessed | tf_op | source)
XLA Modules:
  0.0 86.7 jit_solution(11589834232287043582)
XLA Ops:
  0.6 82.9 %shard_map.119 = (f32[1,32]{1,0:T(1,128)S(1)}, bf16[32,2,1024]{2,1,0:T(2,128)(2,1)S(1)}, f32[1024,640]{1,0:T(8,128)S(1)}, f32[640,640]{1,0:T(8,128)S(1)}, f32[640,1024]{1,0:T(8,128)S(1)}) custom-call(bf16[32,2,1024]{2,1,0:T(2,128)(2,1)} %f_hbm.1, bf16[32,64,640]{2,1,0:T(8,128)(2,1)} %pred_ref.1, bf16[1024,640]{1,0:T(8,128)(2,1)} %we_hbm.1, ...), custom_call_target="tpu_custom_call" | custom-call | tf_op jit(solution)/shard_map/pallas_call | solution.py:619
  83.6 3.0 %shard_map.120 = (f32[1,32]{1,0:T(1,128)}, bf16[32,2,1024]{2,1,0:T(2,128)(2,1)}, f32[1024,640]{1,0:T(8,128)}, f32[640,640]{1,0:T(8,128)}, f32[640,1024]{1,0:T(8,128)}) custom-call(f32[1,32]{1,0:T(1,128)S(1)} %get-tuple-element.15.refs_0_, bf16[32,2,1024]{2,1,0:T(2,128)(2,1)S(1)} %get-tuple-element.16.refs_1_, f32[1024,640]{1,0:T(8,128)S(1)} %get-tuple-element.17.refs_2_, ...), custom_call_target="tpu_custom_call" | custom-call | tf_op jit(solution)/shard_map/pallas_call | solution.py:641

commit v5 on v4

--- a/solution.py
+++ b/solution.py
@@ -272,6 +272,7 @@
 
 
 LEVELS = 3
+MOVE_PARTS = 4
 BLK_G = 2
 
 
@@ -584,7 +585,12 @@
 
 def move(count, *refs):
     src, dst, sem = refs[:count], refs[count:2 * count], refs[2 * count]
-    copies = [pltpu.make_async_copy(a, b, sem.at[k]) for k, (a, b) in enumerate(zip(src, dst))]
+    parts = []
+    for a, b in zip(src, dst):
+        cut = MOVE_PARTS if len(a.shape) == 2 and a.shape[0] % (8 * MOVE_PARTS) == 0 else 1
+        size = a.shape[0] // cut
+        parts += [(a.at[pl.ds(k * size, size)], b.at[pl.ds(k * size, size)]) for k in range(cut)]
+    copies = [pltpu.make_async_copy(a, b, sem.at[k]) for k, (a, b) in enumerate(parts)]
     for cp in copies:
         cp.start()
     for cp in copies:
@@ -635,12 +641,12 @@
                 pltpu.VMEM((2, SIDE, SIDE, m_o, LANES), F32), *ar_scratch(m_o), *ar_scratch(m_p),
                 pltpu.SemaphoreType.DMA((5,)),
                 pltpu.SemaphoreType.DMA, pltpu.SemaphoreType.DMA, pltpu.SemaphoreType.DMA, pltpu.SemaphoreType.DMA,
-                pltpu.SemaphoreType.DMA((48,)), pltpu.SemaphoreType.DMA((n_sem,))],
+                pltpu.SemaphoreType.DMA((32,)), pltpu.SemaphoreType.DMA((n_sem,))],
             compiler_params=pltpu.CompilerParams(collective_id=0, has_side_effects=True, vmem_limit_bytes=57 * 1024 * 1024 - 128 * 1024),
         )(enc_out, pred_out, w_enc, w_pred, w_out, labels, frame_len, label_len)
         loss, genc, gwe, gwp, gwo = pl.pallas_call(
             functools.partial(move, len(shapes)), out_shape=shapes, in_specs=[vm] * len(shapes), out_specs=(hbm,) * len(shapes),
-            scratch_shapes=[pltpu.SemaphoreType.DMA((len(shapes),))], compiler_params=pltpu.CompilerParams(vmem_limit_bytes=256 * 1024))(*outs)
+            scratch_shapes=[pltpu.SemaphoreType.DMA((MOVE_PARTS * len(shapes),))], compiler_params=pltpu.CompilerParams(vmem_limit_bytes=256 * 1024))(*outs)
         return loss.reshape(n), genc, gwe, gwp, gwo
 
     in_specs = (P('dp', 'seq', None), P('dp', None, None), P(None, None), P(None, None), P(None, None), P('dp', None), P('dp'), P('dp'))

time: 86.9 us -> 86.8 us (level)
  no operation moved by 1% of the time
where the time goes in v5:
time: 86.8 us; the launch traced here: 86.7 us
  Pallas kernels  85.8 us (99%)
    pallas_call x1, Pallas kernels, local_fn(): pl.pallas_call(functools.partial(kernel, n), out_shape=tuple((pltpu.VMEM(...  82.8 us
    pallas_call x1, Pallas kernels, local_fn(): pl.pallas_call(functools.partial(move, len(shapes)), out_shape=shapes, in...  3.06 us

profile of v5, /device:TPU:97, one launch (start us, length us, event | category | flops | bytes accessed | tf_op | source)
XLA Modules:
  0.0 86.7 jit_solution(15842294924308293252)
XLA Ops:
  0.6 82.8 %shard_map.119 = (f32[1,32]{1,0:T(1,128)S(1)}, bf16[32,2,1024]{2,1,0:T(2,128)(2,1)S(1)}, f32[1024,640]{1,0:T(8,128)S(1)}, f32[640,640]{1,0:T(8,128)S(1)}, f32[640,1024]{1,0:T(8,128)S(1)}) custom-call(bf16[32,2,1024]{2,1,0:T(2,128)(2,1)} %f_hbm.1, bf16[32,64,640]{2,1,0:T(8,128)(2,1)} %pred_ref.1, bf16[1024,640]{1,0:T(8,128)(2,1)} %we_hbm.1, ...), custom_call_target="tpu_custom_call" | custom-call | tf_op jit(solution)/shard_map/pallas_call | solution.py:625
  83.4 3.1 %shard_map.120 = (f32[1,32]{1,0:T(1,128)}, bf16[32,2,1024]{2,1,0:T(2,128)(2,1)}, f32[1024,640]{1,0:T(8,128)}, f32[640,640]{1,0:T(8,128)}, f32[640,1024]{1,0:T(8,128)}) custom-call(f32[1,32]{1,0:T(1,128)S(1)} %get-tuple-element.15.refs_0_, bf16[32,2,1024]{2,1,0:T(2,128)(2,1)S(1)} %get-tuple-element.16.refs_1_, f32[1024,640]{1,0:T(8,128)S(1)} %get-tuple-element.17.refs_2_, ...), custom_call_target="tpu_custom_call" | custom-call | tf_op jit(solution)/shard_map/pallas_call | solution.py:647
